TPU v7x, 256 devices: a whole 4x4x8 slice. The times are simulated.
256 devices in a mesh: slab: 8 (over z), pencil: 32 (over y, x, core).
Axes of the slice: x: 4, y: 4, z: 8, core: 2. Of those that a mesh axis runs over, the one named last changes fastest.
Arguments:
- right_sides: float32 [8, 128, 128, 128], P(None, 'slab', 'pencil'), may hold values from -6 to 6
- spectrum: float32 [128, 128, 128], P('pencil', 'slab'), may hold values from 0.5 to 20, as said below
- noise_var: float32 [128, 128, 128], P('slab', 'pencil'), may hold values from 0.05 to 1
- observed: int32 [128, 128, 128], P('slab', 'pencil'), may hold values 0 or 1
Outputs:
- solution: float32 [8, 128, 128, 128], P(None, 'slab', 'pencil')
- noise_grad: float32 [128, 128, 128], P('slab', 'pencil')
Inputs may be any that keep to these rules, and one draw needn't show every extreme that they name: Even in every index: spectrum[a, b, c] equals spectrum[(-a) mod 128, (-b) mod 128, (-c) mod 128].
All inputs are finite; a program needn't handle non-finite values. No bound on the sum of `observed` on one device may be relied on, other than what follows from the above.
Results may differ from a plain program's by a relative error of at most 0.00021.
Values sent between devices are 32-bit elements; how exact they have to be, the bound alone decides.
No kernel may reach another device: no remote copies, remote signals or barrier semaphores. Data moves between devices by JAX's collectives and lax.ppermute only.
A program may use at most 64 MiB of HBM per device.

v0:
```python
import functools
import math

import jax
import jax.numpy as jnp
from jax import lax
from jax.sharding import Mesh
from jax.sharding import PartitionSpec as P

NZ = 128
NY = 128
NX = 128
ITERS = 3
PENCIL = ("pencil_0", "pencil_1", "pencil_2")
SLAB_PENCIL = ("slab", "pencil_0", "pencil_1", "pencil_2")


precise = lax.Precision.HIGHEST


def over_axes(value, axes):
    return functools.reduce(lax.psum, axes, value)


def tables(length):
    points = jnp.arange(length, dtype=jnp.int32)
    phase_index = points[:, None] * points[None, :] % length
    angles = phase_index.astype(jnp.float32) * (2.0 * math.pi / length)
    return (jnp.cos(angles), jnp.sin(angles))


def full_table(length, forward):
    cosine, sine_table = tables(length)
    sign_factor = 1.0 if forward else -1.0
    real_row = jnp.stack((cosine, sign_factor * sine_table), axis=1)
    imag_row = jnp.stack((-sign_factor * sine_table, cosine), axis=1)
    return jnp.stack((real_row, imag_row))


def operate(field_block, eigen_block, seen_cells, noise_var):
    masked = field_block * seen_cells
    probe_count, z_local, y_local, extent = masked.shape
    pairs = masked.reshape(probe_count // 2, 2, z_local, y_local, extent)
    spec_x = jnp.einsum("qczyx,dkcx->dkyqz", pairs, full_table(extent, True), precision=precise)
    spec_x = spec_x.reshape(2, extent, y_local, probe_count // 2 * z_local)
    local_probes = spec_x.shape[3] // z_local
    pieces = lax.all_to_all(spec_x, PENCIL, split_axis=1, concat_axis=2, tiled=True)
    row_block = jnp.einsum(
        "ckyr,dmcy->dkmr", pieces, full_table(pieces.shape[2], True), precision=precise
    )
    row_block = row_block.reshape(row_block.shape[:3] + (local_probes, z_local))
    pieces = lax.all_to_all(row_block, "slab", split_axis=2, concat_axis=4, tiled=True)
    length = pieces.shape[4]
    spectral = jnp.einsum("ckjpz,dmcz->dkjpm", pieces, full_table(length, True), precision=precise)
    spectral = spectral * eigen_block[None, :, :, None, :]
    slab_block = jnp.einsum(
        "ckjpm,dzcm->dkjpz", spectral, full_table(length, False), precision=precise
    )
    pieces = lax.all_to_all(slab_block, "slab", split_axis=4, concat_axis=2, tiled=True)
    back_block = jnp.einsum(
        "ckmpz,dycm->dkypz", pieces, full_table(pieces.shape[2], False), precision=precise
    )
    back_block = back_block.reshape(back_block.shape[:3] + (local_probes * z_local,))
    pieces = lax.all_to_all(back_block, PENCIL, split_axis=2, concat_axis=1, tiled=True)
    length = pieces.shape[1]
    smooth = jnp.einsum("ckyr,dxck->rdyx", pieces, full_table(length, False), precision=precise)
    smooth = smooth.reshape(probe_count // 2, z_local, 2, y_local, extent)
    smooth = jnp.transpose(smooth, (0, 2, 1, 3, 4)).reshape(probe_count, z_local, y_local, extent)
    return seen_cells * smooth + noise_var * field_block


def symmetric(matrix):
    return 0.5 * (matrix + matrix.T)


def solve_spd(matrix, right_hand):
    factor = jnp.linalg.cholesky(symmetric(matrix))
    halfway = lax.linalg.triangular_solve(factor, right_hand, left_side=True, lower=True)
    return lax.linalg.triangular_solve(
        factor, halfway, left_side=True, lower=True, transpose_a=True
    )


def gram_local(left, right):
    column_count = left.shape[0]
    return jnp.dot(
        left.reshape(column_count, -1), right.reshape(column_count, -1).T, precision=precise
    )


def combine(field_block, coefficients):
    column_count = field_block.shape[0]
    mixed = jnp.dot(coefficients.T, field_block.reshape(column_count, -1), precision=precise)
    return mixed.reshape(field_block.shape)


def both_grams(residual, image_block):
    return (
        over_axes(gram_local(residual, residual), SLAB_PENCIL),
        over_axes(gram_local(residual, image_block), SLAB_PENCIL),
    )


def local(right_sides, spectrum, noise_var, observed):
    eigen_block = spectrum * (1.0 / (NX * NY * NZ))
    seen_cells = observed.astype(jnp.float32)
    solution = jnp.zeros_like(right_sides)
    residual = right_sides
    image_block = operate(residual, eigen_block, seen_cells, noise_var)
    gamma_now, delta_now = both_grams(residual, image_block)
    direction = residual
    along_image = image_block
    for iteration in range(ITERS):
        alpha_step = solve_spd(delta_now, gamma_now)
        solution = solution + combine(direction, alpha_step)
        if iteration + 1 < ITERS:
            residual = residual - combine(along_image, alpha_step)
            image_block = operate(residual, eigen_block, seen_cells, noise_var)
            gamma_next, product = both_grams(residual, image_block)
            beta_step = solve_spd(gamma_now, gamma_next)
            delta_now = product - jnp.dot(
                jnp.dot(beta_step.T, delta_now.T, precision=precise), beta_step, precision=precise
            )
            direction = residual + combine(direction, beta_step)
            along_image = image_block + combine(along_image, beta_step)
            gamma_now = gamma_next
    weights = right_sides[1:] * solution[1:]
    noise_grad = 0.5 * (solution[0] * solution[0] - jnp.mean(weights, axis=0))
    return (solution, noise_grad)


def solution(mesh):
    split = Mesh(
        mesh.devices.reshape(mesh.shape["slab"], 4, 4, 2),
        ("slab", "pencil_0", "pencil_1", "pencil_2"),
    )
    return jax.shard_map(
        local,
        mesh=split,
        in_specs=(
            P(None, "slab", PENCIL, None),
            P(PENCIL, "slab", None),
            P("slab", PENCIL, None),
            P("slab", PENCIL, None),
        ),
        out_specs=(P(None, "slab", PENCIL, None), P("slab", PENCIL, None)),
        check_vma=False,
    )
```

profile of v0, /device:TPU:1, one launch (start us, length us, event | category | flops | bytes accessed | tf_op | source)
XLA Modules:
  0.0 414.1 jit_solution(11745315092880318477)
XLA Ops:
  5.1 17.2 %all_to_all.216 = f32[32,1,2048]{2,1,0:T(1,128)S(1)} all-to-all(f32[32,1,2048]{2,1,0:T(1,128)S(1)} %reshape.316), channel_id=1, replica_groups=mesh['slab'=8,'pencil_0'=4,'pencil_1'=4,'pencil_2'=2] {'pencil_0','penci..., dimensions={0} | all-to-all | bytes 524288 | tf_op jit(solution)/shard_map/all_to_all | solution.py:47
  29.8 8.4 %all-to-all-start.1 = ((f32[8,1,8192]{2,1,0:T(1,128)}), f32[8,1,8192]{2,1,0:T(1,128)S(1)}, u32[]{:S(2)}, u32[]{:S(2)}) async-start(f32[8,1,8192]{2,1,0:T(1,128)} %reshape.318), calls=%async_computation.1 | async-start | bytes 524288 | tf_op jit(solution)/shard_map/all_to_all | solution.py:52
  38.2 12.2 %all-to-all-done.1 = f32[8,1,8192]{2,1,0:T(1,128)S(1)} async-done(((f32[8,1,8192]{2,1,0:T(1,128)}), f32[8,1,8192]{2,1,0:T(1,128)S(1)}, u32[]{:S(2)}, u32[]{:S(2)}) %all-to-all-start.1) | async-done | bytes 262176 | tf_op jit(solution)/shard_map/all_to_all | solution.py:52
  61.9 14.1 %all_to_all.217 = f32[8,1,8192]{2,1,0:T(1,128)S(1)} all-to-all(f32[8,1,8192]{2,1,0:T(1,128)S(1)} %reshape.320), channel_id=1, replica_groups=mesh['slab'=8,'pencil_0'=4,'pencil_1'=4,'pencil_2'=2] {'slab'}, dimensions={0} | all-to-all | bytes 524288 | tf_op jit(solution)/shard_map/all_to_all | solution.py:59
  85.5 4.9 %all-to-all-start.3 = ((f32[32,1,2048]{2,1,0:T(1,128)}), f32[32,1,2048]{2,1,0:T(1,128)S(1)}, u32[]{:S(2)}, u32[]{:S(2)}) async-start(f32[32,1,2048]{2,1,0:T(1,128)} %reshape.322), calls=%async_computation.3 | async-start | bytes 524288 | tf_op jit(solution)/shard_map/all_to_all | solution.py:64
  91.1 8.3 %all-to-all-done.3 = f32[32,1,2048]{2,1,0:T(1,128)S(1)} async-done(((f32[32,1,2048]{2,1,0:T(1,128)}), f32[32,1,2048]{2,1,0:T(1,128)S(1)}, u32[]{:S(2)}, u32[]{:S(2)}) %all-to-all-start.3) | async-done | bytes 262176 | tf_op jit(solution)/shard_map/all_to_all | solution.py:64
  103.4 11.2 %all-reduce.2 = (f32[8,8]{1,0:T(8,128)S(1)}, f32[8,8]{1,0:T(8,128)S(1)}) all-reduce(f32[8,8]{1,0:T(8,128)S(1)} %convolution_bitcast_fusion.16, f32[8,8]{1,0:T(8,128)S(1)} %convolution_bitcast_fusion.17), channel_id=1, replica_groups=mesh['slab'=8,'pencil_0'=4,'pencil_1'=4,'pencil_2'=2] {'slab'}, use_global_device_ids=true, to_apply=%region_6.8 | all-reduce | flops 128 | bytes 1024 | tf_op jit(solution)/shard_map/psum | solution.py:22
  114.6 7.3 %all-reduce.8 = (f32[8,8]{1,0:T(8,128)S(1)}, f32[8,8]{1,0:T(8,128)S(1)}) all-reduce(f32[8,8]{1,0:T(8,128)S(1)} %get-tuple-element.17, f32[8,8]{1,0:T(8,128)S(1)} %get-tuple-element.18), channel_id=1, replica_groups=mesh['slab'=8,'pencil_0'=4,'pencil_1'=4,'pencil_2'=2] {'pencil_0'}, use_global_device_ids=true, to_apply=%region_7.9 | all-reduce | flops 128 | bytes 1024 | tf_op jit(solution)/shard_map/psum | solution.py:22
  121.9 7.3 %all-reduce.5 = (f32[8,8]{1,0:T(8,128)S(1)}, f32[8,8]{1,0:T(8,128)S(1)}) all-reduce(f32[8,8]{1,0:T(8,128)S(1)} %get-tuple-element.29, f32[8,8]{1,0:T(8,128)S(1)} %get-tuple-element.30), channel_id=1, replica_groups=mesh['slab'=8,'pencil_0'=4,'pencil_1'=4,'pencil_2'=2] {'pencil_1'}, use_global_device_ids=true, to_apply=%region_8.10 | all-reduce | flops 128 | bytes 1024 | tf_op jit(solution)/shard_map/psum | solution.py:22
  129.1 9.6 %all-reduce.11 = (f32[8,8]{1,0:T(8,128)S(1)}, f32[8,8]{1,0:T(8,128)S(1)}) all-reduce(f32[8,8]{1,0:T(8,128)S(1)} %get-tuple-element.23, f32[8,8]{1,0:T(8,128)S(1)} %get-tuple-element.24), channel_id=1, replica_groups=mesh['slab'=8,'pencil_0'=4,'pencil_1'=4,'pencil_2'=2] {'pencil_2'}, use_global_device_ids=true, to_apply=%region_9.11 | all-reduce | flops 128 | bytes 1024 | tf_op jit(solution)/shard_map/psum | solution.py:22
  143.9 12.0 %all_to_all.218 = f32[32,1,2048]{2,1,0:T(1,128)S(1)} all-to-all(f32[32,1,2048]{2,1,0:T(1,128)S(1)} %reshape.324), channel_id=1, replica_groups=mesh['slab'=8,'pencil_0'=4,'pencil_1'=4,'pencil_2'=2] {'pencil_0','penci..., dimensions={0} | all-to-all | bytes 524288 | tf_op jit(solution)/shard_map/all_to_all | solution.py:47
  164.3 3.8 all-to-all-start.5
  168.2 12.1 %all-to-all-done.5 = f32[8,1,8192]{2,1,0:T(1,128)S(1)} async-done(((f32[8,1,8192]{2,1,0:T(1,128)}), f32[8,1,8192]{2,1,0:T(1,128)S(1)}, u32[]{:S(2)}, u32[]{:S(2)}) %all-to-all-start.5) | async-done | bytes 262176 | tf_op jit(solution)/shard_map/all_to_all | solution.py:52
  200.7 10.2 %all-to-all-done.6 = f32[8,1,8192]{2,1,0:T(1,128)S(1)} async-done(((f32[8,1,8192]{2,1,0:T(1,128)}), f32[8,1,8192]{2,1,0:T(1,128)S(1)}, u32[]{:S(2)}, u32[]{:S(2)}) %all-to-all-start.6) | async-done | bytes 262176 | tf_op jit(solution)/shard_map/all_to_all | solution.py:59
  221.9 4.8 %all-to-all-start.7 = ((f32[32,1,2048]{2,1,0:T(1,128)}), f32[32,1,2048]{2,1,0:T(1,128)S(1)}, u32[]{:S(2)}, u32[]{:S(2)}) async-start(f32[32,1,2048]{2,1,0:T(1,128)} %reshape.330), calls=%async_computation.7 | async-start | bytes 524288 | tf_op jit(solution)/shard_map/all_to_all | solution.py:64
  228.6 7.1 %all-to-all-done.7 = f32[32,1,2048]{2,1,0:T(1,128)S(1)} async-done(((f32[32,1,2048]{2,1,0:T(1,128)}), f32[32,1,2048]{2,1,0:T(1,128)S(1)}, u32[]{:S(2)}, u32[]{:S(2)}) %all-to-all-start.7) | async-done | bytes 262176 | tf_op jit(solution)/shard_map/all_to_all | solution.py:64
  239.7 11.2 %all-reduce.1 = (f32[8,8]{1,0:T(8,128)S(1)}, f32[8,8]{1,0:T(8,128)S(1)}) all-reduce(f32[8,8]{1,0:T(8,128)S(1)} %convolution_bitcast_fusion.14, f32[8,8]{1,0:T(8,128)S(1)} %convolution_bitcast_fusion.15), channel_id=1, replica_groups=mesh['slab'=8,'pencil_0'=4,'pencil_1'=4,'pencil_2'=2] {'slab'}, use_global_device_ids=true, to_apply=%region_14.0 | all-reduce | flops 128 | bytes 1024 | tf_op jit(solution)/shard_map/psum | solution.py:22
  250.9 7.3 %all-reduce.7 = (f32[8,8]{1,0:T(8,128)S(1)}, f32[8,8]{1,0:T(8,128)S(1)}) all-reduce(f32[8,8]{1,0:T(8,128)S(1)} %get-tuple-element.15, f32[8,8]{1,0:T(8,128)S(1)} %get-tuple-element.16), channel_id=1, replica_groups=mesh['slab'=8,'pencil_0'=4,'pencil_1'=4,'pencil_2'=2] {'pencil_0'}, use_global_device_ids=true, to_apply=%region_15.0 | all-reduce | flops 128 | bytes 1024 | tf_op jit(solution)/shard_map/psum | solution.py:22
  258.2 7.3 %all-reduce.4 = (f32[8,8]{1,0:T(8,128)S(1)}, f32[8,8]{1,0:T(8,128)S(1)}) all-reduce(f32[8,8]{1,0:T(8,128)S(1)} %get-tuple-element.27, f32[8,8]{1,0:T(8,128)S(1)} %get-tuple-element.28), channel_id=1, replica_groups=mesh['slab'=8,'pencil_0'=4,'pencil_1'=4,'pencil_2'=2] {'pencil_1'}, use_global_device_ids=true, to_apply=%region_16.0 | all-reduce | flops 128 | bytes 1024 | tf_op jit(solution)/shard_map/psum | solution.py:22
  265.5 9.6 %all-reduce.10 = (f32[8,8]{1,0:T(8,128)S(1)}, f32[8,8]{1,0:T(8,128)S(1)}) all-reduce(f32[8,8]{1,0:T(8,128)S(1)} %get-tuple-element.21, f32[8,8]{1,0:T(8,128)S(1)} %get-tuple-element.22), channel_id=1, replica_groups=mesh['slab'=8,'pencil_0'=4,'pencil_1'=4,'pencil_2'=2] {'pencil_2'}, use_global_device_ids=true, to_apply=%region_17.0 | all-reduce | flops 128 | bytes 1024 | tf_op jit(solution)/shard_map/psum | solution.py:22
  281.9 3.9 all-to-all-start.8
  287.0 7.7 %all-to-all-done.8 = f32[32,1,2048]{2,1,0:T(1,128)S(1)} async-done(((f32[32,1,2048]{2,1,0:T(1,128)}), f32[32,1,2048]{2,1,0:T(1,128)S(1)}, u32[]{:S(2)}, u32[]{:S(2)}) %all-to-all-start.8) | async-done | bytes 262176 | tf_op jit(solution)/shard_map/all_to_all | solution.py:47
  301.7 3.6 all-to-all-start.9
  306.8 10.7 %all-to-all-done.9 = f32[8,1,8192]{2,1,0:T(1,128)S(1)} async-done(((f32[8,1,8192]{2,1,0:T(1,128)}), f32[8,1,8192]{2,1,0:T(1,128)S(1)}, u32[]{:S(2)}, u32[]{:S(2)}) %all-to-all-start.9) | async-done | bytes 262176 | tf_op jit(solution)/shard_map/all_to_all | solution.py:52
  329.7 3.7 all-to-all-start.10
  334.4 10.6 %all-to-all-done.10 = f32[8,1,8192]{2,1,0:T(1,128)S(1)} async-done(((f32[8,1,8192]{2,1,0:T(1,128)}), f32[8,1,8192]{2,1,0:T(1,128)S(1)}, u32[]{:S(2)}, u32[]{:S(2)}) %all-to-all-start.10) | async-done | bytes 262176 | tf_op jit(solution)/shard_map/all_to_all | solution.py:59
  354.4 4.6 %all-to-all-start.11 = ((f32[32,1,2048]{2,1,0:T(1,128)}), f32[32,1,2048]{2,1,0:T(1,128)S(1)}, u32[]{:S(2)}, u32[]{:S(2)}) async-start(f32[32,1,2048]{2,1,0:T(1,128)} %reshape.338), calls=%async_computation.11 | async-start | bytes 524288 | tf_op jit(solution)/shard_map/all_to_all | solution.py:64
  360.7 7.3 %all-to-all-done.11 = f32[32,1,2048]{2,1,0:T(1,128)S(1)} async-done(((f32[32,1,2048]{2,1,0:T(1,128)}), f32[32,1,2048]{2,1,0:T(1,128)S(1)}, u32[]{:S(2)}, u32[]{:S(2)}) %all-to-all-start.11) | async-done | bytes 262176 | tf_op jit(solution)/shard_map/all_to_all | solution.py:64
  372.0 11.2 %all-reduce = (f32[8,8]{1,0:T(8,128)S(1)}, f32[8,8]{1,0:T(8,128)S(1)}) all-reduce(f32[8,8]{1,0:T(8,128)S(1)} %convolution_bitcast_fusion.12, f32[8,8]{1,0:T(8,128)S(1)} %convolution_bitcast_fusion.13), channel_id=1, replica_groups=mesh['slab'=8,'pencil_0'=4,'pencil_1'=4,'pencil_2'=2] {'slab'}, use_global_device_ids=true, to_apply=%region_22.0 | all-reduce | flops 128 | bytes 1024 | tf_op jit(solution)/shard_map/psum | solution.py:22
  383.2 7.3 %all-reduce.6 = (f32[8,8]{1,0:T(8,128)S(1)}, f32[8,8]{1,0:T(8,128)S(1)}) all-reduce(f32[8,8]{1,0:T(8,128)S(1)} %get-tuple-element.13, f32[8,8]{1,0:T(8,128)S(1)} %get-tuple-element.14), channel_id=1, replica_groups=mesh['slab'=8,'pencil_0'=4,'pencil_1'=4,'pencil_2'=2] {'pencil_0'}, use_global_device_ids=true, to_apply=%region_23.0 | all-reduce | flops 128 | bytes 1024 | tf_op jit(solution)/shard_map/psum | solution.py:22
  390.5 7.3 %all-reduce.3 = (f32[8,8]{1,0:T(8,128)S(1)}, f32[8,8]{1,0:T(8,128)S(1)}) all-reduce(f32[8,8]{1,0:T(8,128)S(1)} %get-tuple-element.25, f32[8,8]{1,0:T(8,128)S(1)} %get-tuple-element.26), channel_id=1, replica_groups=mesh['slab'=8,'pencil_0'=4,'pencil_1'=4,'pencil_2'=2] {'pencil_1'}, use_global_device_ids=true, to_apply=%region_24.0 | all-reduce | flops 128 | bytes 1024 | tf_op jit(solution)/shard_map/psum | solution.py:22
  397.8 9.6 %all-reduce.9 = (f32[8,8]{1,0:T(8,128)S(1)}, f32[8,8]{1,0:T(8,128)S(1)}) all-reduce(f32[8,8]{1,0:T(8,128)S(1)} %get-tuple-element.19, f32[8,8]{1,0:T(8,128)S(1)} %get-tuple-element.20), channel_id=1, replica_groups=mesh['slab'=8,'pencil_0'=4,'pencil_1'=4,'pencil_2'=2] {'pencil_2'}, use_global_device_ids=true, to_apply=%region_25.29 | all-reduce | flops 128 | bytes 1024 | tf_op jit(solution)/shard_map/psum | solution.py:22
  (196 shorter events, 138.8 us)
Async XLA Ops:
  26.0 12.2 %copy-start.6 = (f32[4,16,128]{2,1,0:T(8,128)S(1)}, f32[4,16,128]{2,1,0:T(8,128)}, u32[]{:S(2)}) copy-start(f32[4,16,128]{2,1,0:T(8,128)} %param.10) | copy-start | bytes 98308
  29.8 20.6 %all-to-all-start.1 = ((f32[8,1,8192]{2,1,0:T(1,128)}), f32[8,1,8192]{2,1,0:T(1,128)S(1)}, u32[]{:S(2)}, u32[]{:S(2)}) async-start(f32[8,1,8192]{2,1,0:T(1,128)} %reshape.318), calls=%async_computation.1 | async-start | bytes 524288 | tf_op jit(solution)/shard_map/all_to_all | solution.py:52
  81.4 9.0 %copy-start = (f32[8,16,4,128]{3,2,1,0:T(4,128)S(1)}, f32[8,16,4,128]{3,2,1,0:T(4,128)}, u32[]{:S(2)}) copy-start(f32[8,16,4,128]{3,2,1,0:T(4,128)} %param.9) | copy-start | bytes 786436
  85.5 13.9 %all-to-all-start.3 = ((f32[32,1,2048]{2,1,0:T(1,128)}), f32[32,1,2048]{2,1,0:T(1,128)S(1)}, u32[]{:S(2)}, u32[]{:S(2)}) async-start(f32[32,1,2048]{2,1,0:T(1,128)} %reshape.322), calls=%async_computation.3 | async-start | bytes 524288 | tf_op jit(solution)/shard_map/all_to_all | solution.py:64
  100.6 2.1 copy-start.5
  164.3 16.0 %all-to-all-start.5 = ((f32[8,1,8192]{2,1,0:T(1,128)}), f32[8,1,8192]{2,1,0:T(1,128)S(1)}, u32[]{:S(2)}, u32[]{:S(2)}) async-start(f32[8,1,8192]{2,1,0:T(1,128)} %reshape.326), calls=%async_computation.5 | async-start | bytes 524288 | tf_op jit(solution)/shard_map/all_to_all | solution.py:52
  195.8 15.1 %all-to-all-start.6 = ((f32[8,1,8192]{2,1,0:T(1,128)}), f32[8,1,8192]{2,1,0:T(1,128)S(1)}, u32[]{:S(2)}, u32[]{:S(2)}) async-start(f32[8,1,8192]{2,1,0:T(1,128)} %reshape.328), calls=%async_computation.6 | async-start | bytes 524288 | tf_op jit(solution)/shard_map/all_to_all | solution.py:59
  221.9 13.8 %all-to-all-start.7 = ((f32[32,1,2048]{2,1,0:T(1,128)}), f32[32,1,2048]{2,1,0:T(1,128)S(1)}, u32[]{:S(2)}, u32[]{:S(2)}) async-start(f32[32,1,2048]{2,1,0:T(1,128)} %reshape.330), calls=%async_computation.7 | async-start | bytes 524288 | tf_op jit(solution)/shard_map/all_to_all | solution.py:64
  281.9 12.9 %all-to-all-start.8 = ((f32[32,1,2048]{2,1,0:T(1,128)}), f32[32,1,2048]{2,1,0:T(1,128)S(1)}, u32[]{:S(2)}, u32[]{:S(2)}) async-start(f32[32,1,2048]{2,1,0:T(1,128)} %reshape.332), calls=%async_computation.8 | async-start | bytes 524288 | tf_op jit(solution)/shard_map/all_to_all | solution.py:47
  285.9 12.0 %copy-start.1 = (f32[8,8192]{1,0:T(8,128)}, f32[8,8192]{1,0:T(8,128)S(1)}, u32[]{:S(2)}) copy-start(f32[8,8192]{1,0:T(8,128)S(1)} %reshape.206) | copy-start | bytes 786436
  301.7 15.8 %all-to-all-start.9 = ((f32[8,1,8192]{2,1,0:T(1,128)}), f32[8,1,8192]{2,1,0:T(1,128)S(1)}, u32[]{:S(2)}, u32[]{:S(2)}) async-start(f32[8,1,8192]{2,1,0:T(1,128)} %reshape.334), calls=%async_computation.9 | async-start | bytes 524288 | tf_op jit(solution)/shard_map/all_to_all | solution.py:52
  325.9 8.1 %copy-start.2 = (f32[8,8192]{1,0:T(8,128)S(1)}, f32[8,8192]{1,0:T(8,128)}, u32[]{:S(2)}) copy-start(f32[8,8192]{1,0:T(8,128)} %copy-done.1) | copy-start | bytes 786436
  329.7 15.3 %all-to-all-start.10 = ((f32[8,1,8192]{2,1,0:T(1,128)}), f32[8,1,8192]{2,1,0:T(1,128)S(1)}, u32[]{:S(2)}, u32[]{:S(2)}) async-start(f32[8,1,8192]{2,1,0:T(1,128)} %reshape.336), calls=%async_computation.10 | async-start | bytes 524288 | tf_op jit(solution)/shard_map/all_to_all | solution.py:59
  352.5 7.8 %copy-start.4 = (f32[8,16,4,128]{3,0,2,1:T(8,128)S(1)}, f32[8,16,4,128]{3,0,2,1:T(8,128)}, u32[]{:S(2)}) copy-start(f32[8,16,4,128]{3,0,2,1:T(8,128)} %fusion.113) | copy-start | bytes 786436
  354.4 13.6 %all-to-all-start.11 = ((f32[32,1,2048]{2,1,0:T(1,128)}), f32[32,1,2048]{2,1,0:T(1,128)S(1)}, u32[]{:S(2)}, u32[]{:S(2)}) async-start(f32[32,1,2048]{2,1,0:T(1,128)} %reshape.338), calls=%async_computation.11 | async-start | bytes 524288 | tf_op jit(solution)/shard_map/all_to_all | solution.py:64
  371.1 41.8 %copy-start.3 = (f32[8,16,4,128]{3,0,2,1:T(8,128)S(1)}, f32[8,16,4,128]{3,0,2,1:T(8,128)}, u32[]{:S(2)}) copy-start(f32[8,16,4,128]{3,0,2,1:T(8,128)} %get-tuple-element.37) | copy-start | bytes 786436
where the time goes:
time: 421 us; the launch traced here: 414 us
  blocking collectives  149 us (35%)
  waiting for transfers between devices  86.2 us (20%)
  local copies, waits for them, and re-layouts  78 us (19%)
  starting transfers between devices  41 us (10%)
  other arithmetic  33.9 us (8%)
  matrix products  23.5 us (6%)
    psum x12, blocking collectives, over_axes(): return functools.reduce(lax.psum, axes, value)  106 us
    all_to_all x3, waiting for transfers between devices, operate(): lax.all_to_all(row_block, 'slab', split_axis=2, concat_axis=4, tiled=True)  35 us
    unnamed x39, local copies, waits for them, and re-layouts  32.3 us
    all_to_all x2, blocking collectives, operate(): lax.all_to_all(spec_x, PENCIL, split_axis=1, concat_axis=2, tiled=True)  29.2 us
    all_to_all x3, waiting for transfers between devices, operate(): lax.all_to_all(back_block, PENCIL, split_axis=2, concat_axis=1, tiled=True)  22.7 us
    all_to_all x2, waiting for transfers between devices, operate(): lax.all_to_all(slab_block, 'slab', split_axis=4, concat_axis=2, tiled=True)  20.8 us
    all_to_all x3, starting transfers between devices, operate(): lax.all_to_all(row_block, 'slab', split_axis=2, concat_axis=4, tiled=True)  15.8 us
    all_to_all x3, starting transfers between devices, operate(): lax.all_to_all(back_block, PENCIL, split_axis=2, concat_axis=1, tiled=True)  14.3 us
  transfers between devices with their start and end apart: 9, of which 9 were waited for; matrix products, arithmetic and copies ran while one was open for 2% of the time, Pallas kernels for 0%

commit v1 on v0

v1 whole, which is shorter than its diff:
```python
import functools

import jax
import jax.numpy as jnp
import numpy as np
from jax import lax
from jax.experimental import pallas as pl
from jax.experimental.pallas import tpu as pltpu
from jax.sharding import PartitionSpec as P

GRID = 128
CELLS = GRID**3
COLUMNS = 8
SLABS = 8
PENCILS = 32
LINES = GRID // PENCILS
DEPTH = GRID // SLABS
ROWS = DEPTH * LINES
BLOCK = PENCILS * 4 * LINES
SHIFT = 6.0
WIDTH = 8.0
F32 = jnp.float32
BF16 = jnp.bfloat16


def slot_frequencies():
    first = np.where(np.arange(PENCILS) < PENCILS // 2, 0, 1)
    return np.arange(PENCILS)[:, None] * LINES + first[:, None] + np.arange(2)[None, :]


def split_table(table):
    high = table.astype(np.float32).astype(jnp.bfloat16)
    low = (table - high.astype(np.float64)).astype(np.float32).astype(jnp.bfloat16)
    return np.stack((high, low))


@functools.cache
def tables():
    points = np.arange(GRID)
    angle = 2.0 * np.pi / GRID * (points[:, None] * points[None, :] % GRID)
    cosine, sine = np.cos(angle), np.sin(angle)
    wave = slot_frequencies().reshape(-1)
    forward_x = np.stack((cosine[wave], -sine[wave]), axis=1)
    inverse_x = np.stack((2.0 * cosine[wave], -2.0 * sine[wave]), axis=1)
    forward_x[0, 1] = cosine[GRID // 2]
    inverse_x[0, 0] = 1.0
    inverse_x[0, 1] = cosine[GRID // 2]
    forward_x = forward_x.reshape(GRID, GRID)
    inverse_x = inverse_x.reshape(GRID, GRID) / (CELLS * WIDTH)
    forward = np.block([[cosine, sine], [-sine, cosine]])
    inverse = np.block([[cosine, -sine], [sine, cosine]])
    order = (
        np.arange(2)[None, :, None] * GRID
        + np.arange(PENCILS)[:, None, None] * LINES
        + np.arange(LINES)[None, None, :]
    ).reshape(-1)
    forward_y = forward[:, order]
    inverse_y = inverse[order, :]
    is_real = (order < GRID)[None, :]
    real_y = np.where(is_real, forward_y, 0.0)
    imag_y = np.where(is_real, 0.0, np.block([[cosine, cosine], [-sine, -sine]])[:, order])
    return (
        split_table(forward_x),
        split_table(inverse_x),
        np.stack([split_table(t) for t in (real_y, imag_y, forward_y, inverse_y)]),
        np.stack([split_table(t) for t in (forward.T, inverse.T)]),
    )


NN = (((1,), (0,)), ((), ()))
NT = (((1,), (1,)), ((), ()))
TN = (((0,), (0,)), ((), ()))


def halves(value):
    high = value.astype(BF16)
    return high, (value - high.astype(F32)).astype(BF16)


def product(left, right, dims):
    dot = functools.partial(lax.dot_general, dimension_numbers=dims, preferred_element_type=F32)
    return dot(left[0], right[0]) + (dot(left[0], right[1]) + dot(left[1], right[0]))


def pair(ref, *index):
    return ref[(*index, 0)], ref[(*index, 1)]


def lines_of(ref, line, start=0):
    return ref[:, pl.ds(start + line, DEPTH, stride=LINES), :].reshape(GRID, GRID)


def forward_x_lines(values, line, table_ref, out_ref):
    out_ref[pl.ds(line, GRID, stride=LINES), :] = product(pair(table_ref), halves(values), NT)


def start_kernel(staged_ref, table_ref, out_ref):
    for line in range(LINES):
        forward_x_lines(lines_of(staged_ref, line), line, table_ref, out_ref)


def spectrum_of(in_ref, slot, y_ref, z_ref, kind):
    block = in_ref[:, slot * 2 * LINES : (slot + 1) * 2 * LINES, :].reshape(2 * GRID, GRID)
    rows = product(pair(y_ref, kind), halves(block), NN)
    rows = jnp.concatenate((rows[:GRID], rows[GRID:]), axis=1)
    waves = product(halves(rows), pair(z_ref, 0), NN)
    return waves[:, :GRID], waves[:, GRID:]


def weighted_slots(in_ref, weights, y_ref, z_ref):
    real_weight, imag_weight, other_weight = weights
    real_re, real_im = spectrum_of(in_ref, 0, y_ref, z_ref, 0)
    imag_re, imag_im = spectrum_of(in_ref, 0, y_ref, z_ref, 1)
    other_re, other_im = spectrum_of(in_ref, 1, y_ref, z_ref, 2)
    return (
        (
            real_weight * real_re - imag_weight * imag_im,
            real_weight * real_im + imag_weight * imag_re,
        ),
        (other_weight * other_re, other_weight * other_im),
    )


def eigen_planes(staged_ref):
    return [
        staged_ref[:, 3 * ROWS + DEPTH * plane : 3 * ROWS + DEPTH * (plane + 1), :].reshape(
            GRID, GRID
        )
        for plane in range(3)
    ]


def middle_kernel(in_ref, staged_ref, y_ref, z_ref, out_ref):
    slots = weighted_slots(in_ref, eigen_planes(staged_ref), y_ref, z_ref)
    for slot, (real, imag) in enumerate(slots):
        waves = jnp.concatenate((real, imag), axis=1)
        rows = product(halves(waves), pair(z_ref, 1), NN)
        rows = jnp.concatenate((rows[:, :GRID], rows[:, GRID:]), axis=0)
        block = product(pair(y_ref, 3), halves(rows), NN)
        out_ref[:, slot * 2 * LINES : (slot + 1) * 2 * LINES, :] = block.reshape(
            PENCILS, 2 * LINES, GRID
        )


def back_kernel(in_ref, staged_ref, last_ref, inverse_ref, forward_ref, field_ref, out_ref):
    for line in range(LINES):
        waves = in_ref[pl.ds(line, GRID, stride=LINES), :]
        smooth = product(halves(waves), pair(inverse_ref), TN)
        seen = lines_of(staged_ref, line, ROWS)
        noise = lines_of(staged_ref, line, 2 * ROWS)
        field = seen * smooth + noise * lines_of(last_ref, line)
        field_ref[:, pl.ds(line, DEPTH, stride=LINES), :] = field.reshape(SLABS, DEPTH, GRID)
        forward_x_lines(field, line, forward_ref, out_ref)


def energy_kernel(in_ref, staged_ref, factor_ref, first_ref, second_ref, y_ref, z_ref, out_ref):
    planes = eigen_planes(staged_ref)
    factors = (factor_ref[0:1], factor_ref[0:1], factor_ref[1:2])
    weights = [jnp.sqrt(plane * factor) for plane, factor in zip(planes, factors)]
    slots = weighted_slots(in_ref, weights, y_ref, z_ref)
    for index, values in enumerate((*slots[0], *slots[1])):
        out_ref[:, index * DEPTH : (index + 1) * DEPTH, :] = values.reshape(SLABS, DEPTH, GRID)
    out_ref[:, ROWS : 2 * ROWS, :] = first_ref[:, :ROWS, :]
    out_ref[:, 2 * ROWS :, :] = second_ref[:, :ROWS, :]


def gram_kernel(in_ref, base_ref, seen_ref, noise_ref, first_ref, second_ref, out_ref):
    hidden = (1.0 - seen_ref[...]) * noise_ref[...]
    hidden_twice = hidden * noise_ref[...]
    for column in range(COLUMNS):
        source = column * 3 * ROWS
        rows = slice(column * ROWS, (column + 1) * ROWS)
        base = base_ref[rows, :]
        first_ref[rows, :] = in_ref[source + ROWS : source + 2 * ROWS, :] + hidden * base
        second_ref[rows, :] = in_ref[source + 2 * ROWS : source + 3 * ROWS, :] + hidden_twice * base
    zeroth, first, second, scaled, waves = [], [], [], [], []
    for row in range(ROWS):
        pick = pl.ds(row, COLUMNS, stride=ROWS)
        zeroth.append(base_ref[pick, :])
        first.append(first_ref[pick, :])
        second.append(second_ref[pick, :])
        scaled.append(second[-1] * noise_ref[row : row + 1, :])
        waves.append(in_ref[pl.ds(row, COLUMNS, stride=3 * ROWS), :])
    zeroth, first, second, scaled, waves = [
        halves(jnp.concatenate(parts, axis=1)) for parts in (zeroth, first, second, scaled, waves)
    ]
    out_ref[...] = jnp.zeros_like(out_ref)
    pairs = (
        (zeroth, zeroth),
        (zeroth, first),
        (first, first),
        (first, second),
        (second, second),
        (second, scaled),
        (waves, waves),
    )
    for index, (left, right) in enumerate(pairs):
        out_ref[:, index * COLUMNS : (index + 1) * COLUMNS] = product(left, right, NT)


def solve_kernel(
    sums_ref, base_ref, first_ref, second_ref, solution_ref, gradient_ref
):
    lanes = lax.broadcasted_iota(jnp.int32, (COLUMNS, GRID), 1)
    moments = sums_ref[0]
    for slab in range(1, SLABS):
        moments = moments + sums_ref[slab]
    last = (lanes >= 5 * COLUMNS) & (lanes < 6 * COLUMNS)
    moments = moments + jnp.where(last, pltpu.roll(moments, GRID - COLUMNS, 1), 0.0)

    def moved(count):
        return moments if count == 0 else pltpu.roll(moments, count * COLUMNS % GRID, 1)

    degree = 3
    size = degree * COLUMNS
    blocks = []
    for step in range(degree):
        operator = WIDTH * moved(GRID // COLUMNS - step - 1) + SHIFT * moved(
            (GRID // COLUMNS - step) % (GRID // COLUMNS)
        )
        blocks.append(jnp.where(lanes < size, operator, moved(degree - step)))
    system = jnp.concatenate(blocks, axis=0)
    rows = lax.broadcasted_iota(jnp.int32, (size, 1), 0)
    for step in range(size):
        pivot_row = system[step : step + 1, :]
        pivot_row = pivot_row / pivot_row[:, step : step + 1]
        reduced = system - system[:, step : step + 1] * pivot_row
        system = jnp.where(rows == step, pivot_row, reduced)
    sources = (base_ref, first_ref, second_ref)
    weighted = jnp.zeros((ROWS, GRID), F32)
    for target in range(COLUMNS):
        total = jnp.zeros((ROWS, GRID), F32)
        for index in range(size):
            block = sources[index // COLUMNS]
            column = index % COLUMNS
            coefficient = system[index : index + 1, size + target : size + target + 1]
            total = total + coefficient * block[column * ROWS : (column + 1) * ROWS, :]
        rows_out = slice(target * ROWS, (target + 1) * ROWS)
        solution_ref[rows_out, :] = total
        if target == 0:
            weighted = total * total
        else:
            share = 1.0 / (COLUMNS - 1)
            weighted = weighted - share * (total * base_ref[rows_out, :])
    gradient_ref[...] = 0.5 * weighted


def call(kernel, *shapes):
    outs = [jax.ShapeDtypeStruct(shape, F32) for shape in shapes]
    return pl.pallas_call(kernel, out_shape=outs if len(outs) > 1 else outs[0])


def exchange(values, axis, count):
    shape = values.shape
    parts = values.reshape(count, -1, shape[-1])
    return lax.all_to_all(parts, axis, 0, 0, tiled=True)


def own_planes(spectrum):
    pencil = lax.axis_index("pencil")
    low = pencil < PENCILS // 2
    first = jnp.where(low, spectrum[0], spectrum[1])
    second = jnp.where(low, spectrum[1], spectrum[2])
    middle = lax.ppermute(spectrum[0], "pencil", [(PENCILS // 2, 0)])
    partner = jnp.where(pencil == 0, middle, first)
    return jnp.stack((first, partner, second)).reshape(-1, GRID)


def local(right_sides, spectrum, noise_var, observed):
    forward_x, inverse_x, y_tables, z_tables = [jnp.asarray(t) for t in tables()]
    base = right_sides.reshape(COLUMNS, ROWS, GRID)
    seen = observed.astype(F32).reshape(ROWS, GRID)
    noise = (noise_var.reshape(ROWS, GRID) - SHIFT) * (1.0 / WIDTH)
    masked = base * seen
    extra = jnp.concatenate((seen, noise, own_planes(spectrum)), axis=0)
    extra = jnp.broadcast_to(extra[None], (SLABS, *extra.shape))
    staged = exchange(jnp.concatenate((masked, extra), axis=1), "slab", SLABS)

    flat = (BLOCK, GRID)
    cube = (SLABS, ROWS, GRID)
    sent = call(start_kernel, flat)(staged, forward_x)
    fields = [staged]
    for _ in range(2):
        parts = exchange(sent, "pencil", PENCILS)
        sent = call(middle_kernel, parts.shape)(parts, staged, y_tables, z_tables)
        parts = exchange(sent, "pencil", PENCILS).reshape(flat)
        field, sent = call(back_kernel, cube, flat)(
            parts, staged, fields[-1], inverse_x, forward_x
        )
        fields.append(field)
    parts = exchange(sent, "pencil", PENCILS)
    share = 2.0 / (CELLS * WIDTH)
    single = jnp.where(lax.axis_index("pencil") == 0, 0.5 * share, share)
    factors = jnp.broadcast_to(jnp.stack((single, jnp.float32(share)))[:, None], (2, GRID))
    merged = call(energy_kernel, (SLABS, 3 * ROWS, GRID))(
        parts, staged, factors, fields[1], fields[2], y_tables, z_tables
    )
    merged = exchange(merged, "slab", SLABS).reshape(-1, GRID)
    base = base.reshape(flat)
    first, second, sums = call(gram_kernel, flat, flat, (COLUMNS, GRID))(
        merged, base, seen, noise
    )
    sums = exchange(jnp.broadcast_to(sums[None], (PENCILS, COLUMNS, GRID)), "pencil", PENCILS)
    sums = jnp.sum(sums, axis=0)
    sums = exchange(jnp.broadcast_to(sums[None], (SLABS, COLUMNS, GRID)), "slab", SLABS)
    solution, gradient = call(solve_kernel, flat, (ROWS, GRID))(sums, base, first, second)
    return solution.reshape(right_sides.shape), gradient.reshape(noise_var.shape)


def solution(mesh):
    return jax.shard_map(
        local,
        mesh=mesh,
        in_specs=(
            P(None, "slab", "pencil", None),
            P("pencil", "slab", None),
            P("slab", "pencil", None),
            P("slab", "pencil", None),
        ),
        out_specs=(P(None, "slab", "pencil", None), P("slab", "pencil", None)),
        check_vma=False,
    )
```

time: 421 us -> 190 us (0.45); the launches traced: 414 us -> 189 us
  waiting for transfers between devices: 86.2 us -> 8.81 us
  local copies, waits for them, and re-layouts: 78 us -> 2.17 us
  starting transfers between devices: 41 us -> 4.41 us
  other arithmetic: 33.9 us -> 1.94 us
  Pallas kernels: 0 us -> 28.9 us
  matrix products: 23.5 us -> 0 us
  blocking collectives: 149 us -> 142 us
    psum x12 -> x0, blocking collectives: 106 us -> none  [over_axes(): return functools.reduce(lax.psum, axes, value)]
    all_to_all x3 -> x8, blocking collectives: 43.3 us -> 142 us  [exchange(): return lax.all_to_all(parts, axis, 0, 0, tiled=True)]
    all_to_all x9 -> x1, waiting for transfers between devices: 86.2 us -> 8.81 us  [exchange(): return lax.all_to_all(parts, axis, 0, 0, tiled=True)]
    all_to_all x9 -> x1, starting transfers between devices: 41 us -> 3.76 us  [exchange(): return lax.all_to_all(parts, axis, 0, 0, tiled=True)]
    all_to_all x25 -> x0, local copies, waits for them, and re-layouts: 31.6 us -> none  [the longest x6 14.3 us: operate(): lax.all_to_all(slab_block, 'slab', split_axis=4, concat_axis=2, tiled=True)]
    unnamed x39 -> x12, local copies, waits for them, and re-layouts: 32.3 us -> 0.77 us
    pallas_call x0 -> x8, Pallas kernels: none -> 28.9 us  [the longest x2 7.89 us: local(): sent = call(middle_kernel, parts.shape)(parts, staged, y_tables, z_tables)]
    dot_general x36 -> x0, matrix products: 21.6 us -> none  [the longest x8 4.21 us: combine(): jnp.dot(coefficients.T, field_block.reshape(column_count, -1), precision=...]
  transfers between devices with their start and end apart: 9 -> 2, of which waited for: 9 -> 1; matrix products, arithmetic and copies ran while one was open for 2% -> 1% of each run, Pallas kernels for 0% -> 0%
where the time goes in v1:
time: 190 us; the launch traced here: 189 us
  blocking collectives  142 us (75%)
  Pallas kernels  28.9 us (15%)
  waiting for transfers between devices  8.81 us (5%)
  starting transfers between devices  4.41 us (2%)
  local copies, waits for them, and re-layouts  2.17 us (1%)
  other arithmetic  1.94 us (1%)
    all_to_all x8, blocking collectives, exchange(): return lax.all_to_all(parts, axis, 0, 0, tiled=True)  142 us
    all_to_all x1, waiting for transfers between devices, exchange(): return lax.all_to_all(parts, axis, 0, 0, tiled=True)  8.81 us
    pallas_call x2, Pallas kernels, local(): sent = call(middle_kernel, parts.shape)(parts, staged, y_tables, z_tables)  7.89 us
    pallas_call x2, Pallas kernels, local(): call(back_kernel, cube, flat)  5.86 us
    pallas_call x1, Pallas kernels, local(): call(solve_kernel, flat, (ROWS, GRID))(sums, base, first, second)  4.61 us
    pallas_call x1, Pallas kernels, local(): call(gram_kernel, flat, flat, (COLUMNS, GRID))(merged, base, seen, noise)  4.4 us
    pallas_call x1, Pallas kernels, local(): call(energy_kernel, (SLABS, 3 * ROWS, GRID))  3.81 us
  transfers between devices with their start and end apart: 2, of which 1 were waited for; matrix products, arithmetic and copies ran while one was open for 1% of the time, Pallas kernels for 0%

profile of v1, /device:TPU:1, one launch (start us, length us, event | category | flops | bytes accessed | tf_op | source)
XLA Modules:
  0.0 189.2 jit_solution(152244029782590668)
XLA Ops:
  0.6 0.7 slice_select_fusion.1
  1.4 0.6 collective-permute-start
  2.1 0.0 copy-start.1
  2.1 0.0 copy-start.5
  2.1 1.0 broadcast_multiply_fusion
  3.1 0.0 copy-start.3
  3.1 0.0 collective-permute-done
  3.1 0.7 copy-done.3
  3.9 0.0 copy-done.2
  3.9 0.1 pad_maximum_fusion
  4.0 30.1 %all_to_all.45.staged_ref.last_ref = f32[8,240,128]{2,1,0:T(8,128)} all-to-all(f32[8,240,128]{2,1,0:T(8,128)S(1)} %pad_maximum_fusion), channel_id=1, replica_groups=mesh['slab'=8,'pencil'=32] {'slab'}, dimensions={0} | all-to-all | bytes 1966080 | tf_op jit(solution)/shard_map/all_to_all | solution.py:256
  34.1 2.3 %shard_map.95 = f32[512,128]{1,0:T(8,128)} custom-call(f32[8,240,128]{2,1,0:T(8,128)} %all_to_all.45.staged_ref.last_ref, bf16[2,128,128]{2,1,0:T(8,128)(2,1)} %constant.29.clone.table_ref.forward_ref), custom_call_target="tpu_custom_call" | custom-call | tf_op jit(solution)/shard_map/pallas_call | solution.py:281
  36.4 23.1 %all_to_all.46.in_ref = f32[32,16,128]{2,1,0:T(8,128)} all-to-all(f32[32,16,128]{2,1,0:T(8,128)} %bitcast.32), channel_id=1, replica_groups=mesh['slab'=8,'pencil'=32] {'pencil'}, dimensions={0} | all-to-all | bytes 524288 | tf_op jit(solution)/shard_map/all_to_all | solution.py:256
  59.6 3.9 %shard_map.96 = f32[32,16,128]{2,1,0:T(8,128)} custom-call(f32[32,16,128]{2,1,0:T(8,128)} %all_to_all.46.in_ref, f32[8,240,128]{2,1,0:T(8,128)} %all_to_all.45.staged_ref.last_ref, bf16[4,2,256,256]{3,2,1,0:T(8,128)(2,1)} %constant.31.clone.y_ref, bf16[2,2,256,256]{3,2,1,0:T(8,128)(2,1)} %constant.32.clone.z_ref), custom_call_target="tpu_custom_call" | custom-call | tf_op jit(solution)/shard_map/pallas_call | solution.py:285
  63.5 13.3 %all_to_all.47 = f32[32,16,128]{2,1,0:T(8,128)} all-to-all(f32[32,16,128]{2,1,0:T(8,128)} %shard_map.96), channel_id=1, replica_groups=mesh['slab'=8,'pencil'=32] {'pencil'}, dimensions={0} | all-to-all | bytes 524288 | tf_op jit(solution)/shard_map/all_to_all | solution.py:256
  76.8 3.1 %shard_map.97 = (f32[8,64,128]{2,1,0:T(8,128)}, f32[512,128]{1,0:T(8,128)}) custom-call(f32[512,128]{1,0:T(8,128)} %bitcast.31, f32[8,240,128]{2,1,0:T(8,128)} %all_to_all.45.staged_ref.last_ref, f32[8,240,128]{2,1,0:T(8,128)} %all_to_all.45.staged_ref.last_ref, bf16[2,128,128]{2,1,0:T(8,128)(2,1)} %constant.30.clone.inverse_ref, ...), custom_call_target="tpu_custom_call" | custom-call | tf_op jit(solution)/shard_map/pallas_call | solution.py:287
  79.9 13.3 %all_to_all.48.in_ref = f32[32,16,128]{2,1,0:T(8,128)} all-to-all(f32[32,16,128]{2,1,0:T(8,128)} %bitcast.39), channel_id=1, replica_groups=mesh['slab'=8,'pencil'=32] {'pencil'}, dimensions={0} | all-to-all | bytes 524288 | tf_op jit(solution)/shard_map/all_to_all | solution.py:256
  93.2 3.9 %shard_map.98 = f32[32,16,128]{2,1,0:T(8,128)} custom-call(f32[32,16,128]{2,1,0:T(8,128)} %all_to_all.48.in_ref, f32[8,240,128]{2,1,0:T(8,128)} %all_to_all.45.staged_ref.last_ref, bf16[4,2,256,256]{3,2,1,0:T(8,128)(2,1)} %constant.31.clone.y_ref, bf16[2,2,256,256]{3,2,1,0:T(8,128)(2,1)} %constant.32.clone.z_ref), custom_call_target="tpu_custom_call" | custom-call | tf_op jit(solution)/shard_map/pallas_call | solution.py:285
  97.2 13.3 %all_to_all.49 = f32[32,16,128]{2,1,0:T(8,128)} all-to-all(f32[32,16,128]{2,1,0:T(8,128)} %shard_map.98), channel_id=1, replica_groups=mesh['slab'=8,'pencil'=32] {'pencil'}, dimensions={0} | all-to-all | bytes 524288 | tf_op jit(solution)/shard_map/all_to_all | solution.py:256
  110.5 2.8 %shard_map.99 = (f32[8,64,128]{2,1,0:T(8,128)}, f32[512,128]{1,0:T(8,128)}) custom-call(f32[512,128]{1,0:T(8,128)} %bitcast.30, f32[8,240,128]{2,1,0:T(8,128)} %all_to_all.45.staged_ref.last_ref, f32[8,64,128]{2,1,0:T(8,128)} %get-tuple-element.12.last_ref.first_ref, bf16[2,128,128]{2,1,0:T(8,128)(2,1)} %constant.30.clone.inverse_ref, ...), custom_call_target="tpu_custom_call" | custom-call | tf_op jit(solution)/shard_map/pallas_call | solution.py:287
  113.3 3.8 %all-to-all-start.5 = ((f32[32,16,128]{2,1,0:T(8,128)}), f32[32,16,128]{2,1,0:T(8,128)S(1)}, u32[]{:S(2)}, u32[]{:S(2)}) async-start(f32[32,16,128]{2,1,0:T(8,128)} %bitcast.38), calls=%async_computation.5 | async-start | bytes 524288 | tf_op jit(solution)/shard_map/all_to_all | solution.py:256
  117.1 0.1 pad_maximum_fusion.3
  117.2 8.8 %all-to-all-done.5.in_ref = f32[32,16,128]{2,1,0:T(8,128)S(1)} async-done(((f32[32,16,128]{2,1,0:T(8,128)}), f32[32,16,128]{2,1,0:T(8,128)S(1)}, u32[]{:S(2)}, u32[]{:S(2)}) %all-to-all-start.5) | async-done | bytes 262176 | tf_op jit(solution)/shard_map/all_to_all | solution.py:256
  126.0 0.6 broadcast_in_dim.9.factor_ref
  126.6 0.0 copy-done
  126.7 3.8 %shard_map.100 = f32[8,192,128]{2,1,0:T(8,128)} custom-call(f32[32,16,128]{2,1,0:T(8,128)} %copy-done, f32[8,240,128]{2,1,0:T(8,128)} %all_to_all.45.staged_ref.last_ref, f32[2,128]{1,0:T(2,128)} %broadcast_in_dim.9.factor_ref, f32[8,64,128]{2,1,0:T(8,128)} %get-tuple-element.12.last_ref.first_ref, f32[8,64,128]{2,1,0:T(8,128)} %get-tuple-element.14.second_ref, ...), custom_call_target="tpu_custom_call" | custom-call | tf_op jit(solution)/shard_map/pallas_call | solution.py:295
  130.5 27.8 %all_to_all.50 = f32[8,192,128]{2,1,0:T(8,128)} all-to-all(f32[8,192,128]{2,1,0:T(8,128)} %shard_map.100), channel_id=1, replica_groups=mesh['slab'=8,'pencil'=32] {'slab'}, dimensions={0} | all-to-all | bytes 1572864 | tf_op jit(solution)/shard_map/all_to_all | solution.py:256
  158.3 4.4 %shard_map.101 = (f32[512,128]{1,0:T(8,128)}, f32[512,128]{1,0:T(8,128)}, f32[8,128]{1,0:T(8,128)}) custom-call(f32[1536,128]{1,0:T(8,128)} %bitcast.26, f32[512,128]{1,0:T(8,128)} %bitcast.28, f32[64,128]{1,0:T(8,128)} %bitcast.35, f32[64,128]{1,0:T(8,128)} %bitcast.37), custom_call_target="tpu_custom_call" | custom-call | tf_op jit(solution)/shard_map/pallas_call | solution.py:300
  162.7 0.7 broadcast_in_dim.10
  163.4 11.3 %all_to_all.51 = f32[32,8,128]{2,1,0:T(8,128)S(1)} all-to-all(f32[32,8,128]{2,1,0:T(8,128)S(1)} %broadcast_in_dim.10), channel_id=1, replica_groups=mesh['slab'=8,'pencil'=32] {'pencil'}, dimensions={0} | all-to-all | bytes 262144 | tf_op jit(solution)/shard_map/all_to_all | solution.py:256
  174.7 9.9 %all_to_all.52.sums_ref = f32[8,8,128]{2,1,0:T(8,128)} all-to-all(f32[8,8,128]{2,1,0:T(8,128)S(1)} %broadcast_in_dim.11), channel_id=1, replica_groups=mesh['slab'=8,'pencil'=32] {'slab'}, dimensions={0} | all-to-all | bytes 65536 | tf_op jit(solution)/shard_map/all_to_all | solution.py:256
  184.6 4.6 %shard_map.102 = (f32[512,128]{1,0:T(8,128)}, f32[64,128]{1,0:T(8,128)}) custom-call(f32[8,8,128]{2,1,0:T(8,128)} %all_to_all.52.sums_ref, f32[512,128]{1,0:T(8,128)} %bitcast.29, f32[512,128]{1,0:T(8,128)} %get-tuple-element.16.first_ref, f32[512,128]{1,0:T(8,128)} %get-tuple-element.17.second_ref), custom_call_target="tpu_custom_call" | custom-call | tf_op jit(solution)/shard_map/pallas_call | solution.py:306
  (14 shorter events, 0.1 us)
Async XLA Ops:
  0.6 1.4 copy-start.4
  1.4 1.8 collective-permute-start
  2.1 1.8 copy-start.1
  2.1 1.0 copy-start.5
  3.1 0.8 copy-start.3
  3.1 0.7 copy-start.2
  113.3 12.7 %all-to-all-start.5 = ((f32[32,16,128]{2,1,0:T(8,128)}), f32[32,16,128]{2,1,0:T(8,128)S(1)}, u32[]{:S(2)}, u32[]{:S(2)}) async-start(f32[32,16,128]{2,1,0:T(8,128)} %bitcast.38), calls=%async_computation.5 | async-start | bytes 524288 | tf_op jit(solution)/shard_map/all_to_all | solution.py:256
  126.0 0.7 copy-start

commit v2 on v1

--- a/solution.py
+++ b/solution.py
@@ -121,17 +121,20 @@
     )
 
 
-def eigen_planes(staged_ref):
-    return [
-        staged_ref[:, 3 * ROWS + DEPTH * plane : 3 * ROWS + DEPTH * (plane + 1), :].reshape(
-            GRID, GRID
-        )
-        for plane in range(3)
-    ]
-
-
-def middle_kernel(in_ref, staged_ref, y_ref, z_ref, out_ref):
-    slots = weighted_slots(in_ref, eigen_planes(staged_ref), y_ref, z_ref)
+def plane_of(staged_ref, plane):
+    start = 3 * ROWS + DEPTH * plane
+    return staged_ref[:, start : start + DEPTH, :].reshape(GRID, GRID)
+
+
+def eigen_planes(staged_ref, edge_ref):
+    first = plane_of(staged_ref, 0)
+    alone = lax.axis_index("pencil") == 0
+    partner = jnp.where(alone, edge_ref[...], first)
+    return alone, (first, partner, plane_of(staged_ref, 1))
+
+
+def middle_kernel(in_ref, staged_ref, edge_ref, y_ref, z_ref, out_ref):
+    slots = weighted_slots(in_ref, eigen_planes(staged_ref, edge_ref)[1], y_ref, z_ref)
     for slot, (real, imag) in enumerate(slots):
         waves = jnp.concatenate((real, imag), axis=1)
         rows = product(halves(waves), pair(z_ref, 1), NN)
@@ -153,9 +156,11 @@
         forward_x_lines(field, line, forward_ref, out_ref)
 
 
-def energy_kernel(in_ref, staged_ref, factor_ref, first_ref, second_ref, y_ref, z_ref, out_ref):
-    planes = eigen_planes(staged_ref)
-    factors = (factor_ref[0:1], factor_ref[0:1], factor_ref[1:2])
+def energy_kernel(in_ref, staged_ref, edge_ref, first_ref, second_ref, y_ref, z_ref, out_ref):
+    alone, planes = eigen_planes(staged_ref, edge_ref)
+    share = 2.0 / (CELLS * WIDTH)
+    single = jnp.where(alone, 0.5 * share, share)
+    factors = (single, single, share)
     weights = [jnp.sqrt(plane * factor) for plane, factor in zip(planes, factors)]
     slots = weighted_slots(in_ref, weights, y_ref, z_ref)
     for index, values in enumerate((*slots[0], *slots[1])):
@@ -245,9 +250,38 @@
     gradient_ref[...] = 0.5 * weighted
 
 
-def call(kernel, *shapes):
-    outs = [jax.ShapeDtypeStruct(shape, F32) for shape in shapes]
-    return pl.pallas_call(kernel, out_shape=outs if len(outs) > 1 else outs[0])
+def stage_kernel(base_ref, observed_ref, noise_ref, spectrum_ref, out_ref, seen_ref, shifted_ref):
+    seen = observed_ref[...].astype(F32)
+    shifted = (noise_ref[...] - SHIFT) * (1.0 / WIDTH)
+    seen_ref[...] = seen
+    shifted_ref[...] = shifted
+    low = lax.axis_index("pencil") < PENCILS // 2
+    first = jnp.where(low, spectrum_ref[0], spectrum_ref[1])
+    second = jnp.where(low, spectrum_ref[1], spectrum_ref[2])
+    parts = (seen, shifted, first, second, spectrum_ref[0])
+    for slab in range(SLABS):
+        out_ref[slab, :ROWS, :] = base_ref[slab] * seen
+        start = ROWS
+        for part in parts:
+            out_ref[slab, start : start + part.shape[0], :] = part
+            start += part.shape[0]
+
+
+def call(kernel, *shapes, inputs=True, outputs=True):
+    kind = pltpu.VMEM if outputs else jax.ShapeDtypeStruct
+    outs = [kind(shape, F32) for shape in shapes]
+    run = pl.pallas_call(
+        kernel,
+        out_shape=outs if len(outs) > 1 else outs[0],
+        compiler_params=pltpu.CompilerParams(vmem_limit_bytes=24 * 2**20),
+    )
+
+    def placed(*values):
+        if inputs:
+            values = [pltpu.with_memory_space_constraint(value, pltpu.VMEM) for value in values]
+        return run(*values)
+
+    return placed
 
 
 def exchange(values, axis, count):
@@ -256,54 +290,48 @@
     return lax.all_to_all(parts, axis, 0, 0, tiled=True)
 
 
-def own_planes(spectrum):
-    pencil = lax.axis_index("pencil")
-    low = pencil < PENCILS // 2
-    first = jnp.where(low, spectrum[0], spectrum[1])
-    second = jnp.where(low, spectrum[1], spectrum[2])
-    middle = lax.ppermute(spectrum[0], "pencil", [(PENCILS // 2, 0)])
-    partner = jnp.where(pencil == 0, middle, first)
-    return jnp.stack((first, partner, second)).reshape(-1, GRID)
-
-
 def local(right_sides, spectrum, noise_var, observed):
     forward_x, inverse_x, y_tables, z_tables = [jnp.asarray(t) for t in tables()]
-    base = right_sides.reshape(COLUMNS, ROWS, GRID)
-    seen = observed.astype(F32).reshape(ROWS, GRID)
-    noise = (noise_var.reshape(ROWS, GRID) - SHIFT) * (1.0 / WIDTH)
-    masked = base * seen
-    extra = jnp.concatenate((seen, noise, own_planes(spectrum)), axis=0)
-    extra = jnp.broadcast_to(extra[None], (SLABS, *extra.shape))
-    staged = exchange(jnp.concatenate((masked, extra), axis=1), "slab", SLABS)
-
     flat = (BLOCK, GRID)
     cube = (SLABS, ROWS, GRID)
+    square = (ROWS, GRID)
+    staged, seen, noise = call(
+        stage_kernel, (SLABS, 3 * ROWS + 3 * DEPTH, GRID), square, square, inputs=False
+    )(
+        right_sides.reshape(cube),
+        observed.reshape(square),
+        noise_var.reshape(square),
+        spectrum,
+    )
+    staged = exchange(staged, "slab", SLABS)
+    edge = staged[:, 3 * ROWS + 2 * DEPTH :, :].reshape(GRID, GRID)
+    edge = lax.ppermute(edge, "pencil", [(PENCILS // 2, 0)])
+
     sent = call(start_kernel, flat)(staged, forward_x)
     fields = [staged]
     for _ in range(2):
         parts = exchange(sent, "pencil", PENCILS)
-        sent = call(middle_kernel, parts.shape)(parts, staged, y_tables, z_tables)
+        sent = call(middle_kernel, parts.shape)(parts, staged, edge, y_tables, z_tables)
         parts = exchange(sent, "pencil", PENCILS).reshape(flat)
         field, sent = call(back_kernel, cube, flat)(
             parts, staged, fields[-1], inverse_x, forward_x
         )
         fields.append(field)
     parts = exchange(sent, "pencil", PENCILS)
-    share = 2.0 / (CELLS * WIDTH)
-    single = jnp.where(lax.axis_index("pencil") == 0, 0.5 * share, share)
-    factors = jnp.broadcast_to(jnp.stack((single, jnp.float32(share)))[:, None], (2, GRID))
     merged = call(energy_kernel, (SLABS, 3 * ROWS, GRID))(
-        parts, staged, factors, fields[1], fields[2], y_tables, z_tables
+        parts, staged, edge, fields[1], fields[2], y_tables, z_tables
     )
     merged = exchange(merged, "slab", SLABS).reshape(-1, GRID)
-    base = base.reshape(flat)
+    base = right_sides.reshape(flat)
     first, second, sums = call(gram_kernel, flat, flat, (COLUMNS, GRID))(
         merged, base, seen, noise
     )
     sums = exchange(jnp.broadcast_to(sums[None], (PENCILS, COLUMNS, GRID)), "pencil", PENCILS)
     sums = jnp.sum(sums, axis=0)
     sums = exchange(jnp.broadcast_to(sums[None], (SLABS, COLUMNS, GRID)), "slab", SLABS)
-    solution, gradient = call(solve_kernel, flat, (ROWS, GRID))(sums, base, first, second)
+    solution, gradient = call(solve_kernel, flat, (ROWS, GRID), outputs=False)(
+        sums, base, first, second
+    )
     return solution.reshape(right_sides.shape), gradient.reshape(noise_var.shape)
 
 

time: 190 us -> 167 us (0.88)
  Pallas kernels: 28.9 us -> 12.7 us
  blocking collectives: 142 us -> 132 us
  starting transfers between devices: 4.41 us -> 10.1 us
    pallas_call x8 -> x9, Pallas kernels: 28.9 us -> 12.7 us  [placed(): return run(*values)]
    all_to_all x8, blocking collectives: 142 us -> 132 us  [exchange(): return lax.all_to_all(parts, axis, 0, 0, tiled=True)]
    all_to_all x1, starting transfers between devices: 3.76 us -> 9.46 us  [exchange(): return lax.all_to_all(parts, axis, 0, 0, tiled=True)]
    unnamed x12 -> x18, local copies, waits for them, and re-layouts: 0.77 us -> 3.24 us
  transfers between devices with their start and end apart: 2 -> 2, of which waited for: 1 -> 1; matrix products, arithmetic and copies ran while one was open for 1% -> 0% of each run, Pallas kernels for 0% -> 0%
where the time goes in v2:
time: 167 us
  blocking collectives  132 us (79%)
  Pallas kernels  12.7 us (8%)
  starting transfers between devices  10.1 us (6%)
  waiting for transfers between devices  8.18 us (5%)
  local copies, waits for them, and re-layouts  3.29 us (2%)
    all_to_all x8, blocking collectives, exchange(): return lax.all_to_all(parts, axis, 0, 0, tiled=True)  132 us
    pallas_call x9, Pallas kernels, placed(): return run(*values)  12.7 us
    all_to_all x1, starting transfers between devices, exchange(): return lax.all_to_all(parts, axis, 0, 0, tiled=True)  9.46 us
    all_to_all x1, waiting for transfers between devices, exchange(): return lax.all_to_all(parts, axis, 0, 0, tiled=True)  8.18 us
  transfers between devices with their start and end apart: 2, of which 1 were waited for; matrix products, arithmetic and copies ran while one was open for 0% of the time, Pallas kernels for 0%

profile of v2, /device:TPU:1, one launch (start us, length us, event | category | flops | bytes accessed | tf_op | source)
XLA Modules:
  0.0 166.6 jit_solution(11699751370098801741)
XLA Ops:
  0.6 0.0 copy-start.2
  0.6 0.9 copy-done.2
  1.6 0.8 copy-done.6
  2.3 0.8 copy-done.7
  3.1 0.8 copy-done.8
  3.9 0.1 shard_map.95
  3.9 0.0 copy-start.4
  3.9 35.0 %all_to_all.45.staged_ref.last_ref = f32[8,240,128]{2,1,0:T(8,128)S(1)} all-to-all(f32[8,240,128]{2,1,0:T(8,128)S(1)} %get-tuple-element.14), channel_id=1, replica_groups=mesh['slab'=8,'pencil'=32] {'slab'}, dimensions={0} | all-to-all | bytes 1966080 | tf_op jit(solution)/shard_map/all_to_all | solution.py:290
  38.9 0.0 copy-done.4
  38.9 1.1 shard_map.96
  40.0 9.5 %all-to-all-start.1 = ((f32[32,16,128]{2,1,0:T(8,128)}), f32[32,16,128]{2,1,0:T(8,128)S(1)}, u32[]{:S(2)}, u32[]{:S(2)}) async-start(f32[32,16,128]{2,1,0:T(8,128)} %bitcast.3), calls=%async_computation.1 | async-start | bytes 524288 | tf_op jit(solution)/shard_map/all_to_all | solution.py:290
  49.5 0.7 collective-permute-start
  50.2 0.0 collective-permute-done.edge_ref
  50.2 8.2 %all-to-all-done.1.in_ref = f32[32,16,128]{2,1,0:T(8,128)S(1)} async-done(((f32[32,16,128]{2,1,0:T(8,128)}), f32[32,16,128]{2,1,0:T(8,128)S(1)}, u32[]{:S(2)}, u32[]{:S(2)}) %all-to-all-start.1) | async-done | bytes 262176 | tf_op jit(solution)/shard_map/all_to_all | solution.py:290
  58.4 0.0 copy-done
  58.4 0.0 copy-done.1
  58.4 1.5 shard_map.97
  59.9 0.0 copy-start.5
  59.9 12.6 %all_to_all.46 = f32[32,16,128]{2,1,0:T(8,128)S(1)} all-to-all(f32[32,16,128]{2,1,0:T(8,128)S(1)} %shard_map.97), channel_id=1, replica_groups=mesh['slab'=8,'pencil'=32] {'pencil'}, dimensions={0} | all-to-all | bytes 524288 | tf_op jit(solution)/shard_map/all_to_all | solution.py:290
  72.5 0.7 shard_map.98
  73.2 12.4 %all_to_all.47.in_ref = f32[32,16,128]{2,1,0:T(8,128)S(1)} all-to-all(f32[32,16,128]{2,1,0:T(8,128)S(1)} %bitcast.20), channel_id=1, replica_groups=mesh['slab'=8,'pencil'=32] {'pencil'}, dimensions={0} | all-to-all | bytes 524288 | tf_op jit(solution)/shard_map/all_to_all | solution.py:290
  85.6 1.5 shard_map.99
  87.2 12.4 %all_to_all.48 = f32[32,16,128]{2,1,0:T(8,128)S(1)} all-to-all(f32[32,16,128]{2,1,0:T(8,128)S(1)} %shard_map.99), channel_id=1, replica_groups=mesh['slab'=8,'pencil'=32] {'pencil'}, dimensions={0} | all-to-all | bytes 524288 | tf_op jit(solution)/shard_map/all_to_all | solution.py:290
  99.6 0.7 shard_map.100
  100.3 12.4 %all_to_all.49.in_ref = f32[32,16,128]{2,1,0:T(8,128)S(1)} all-to-all(f32[32,16,128]{2,1,0:T(8,128)S(1)} %bitcast.19), channel_id=1, replica_groups=mesh['slab'=8,'pencil'=32] {'pencil'}, dimensions={0} | all-to-all | bytes 524288 | tf_op jit(solution)/shard_map/all_to_all | solution.py:290
  112.8 1.0 shard_map.101
  113.8 0.0 copy-start.3
  113.8 26.2 %all_to_all.50 = f32[8,192,128]{2,1,0:T(8,128)S(1)} all-to-all(f32[8,192,128]{2,1,0:T(8,128)S(1)} %shard_map.101), channel_id=1, replica_groups=mesh['slab'=8,'pencil'=32] {'slab'}, dimensions={0} | all-to-all | bytes 1572864 | tf_op jit(solution)/shard_map/all_to_all | solution.py:290
  139.9 2.6 %shard_map.102 = (f32[512,128]{1,0:T(8,128)S(1)}, f32[512,128]{1,0:T(8,128)S(1)}, f32[8,128]{1,0:T(8,128)S(1)}) custom-call(f32[1536,128]{1,0:T(8,128)S(1)} %bitcast.13, f32[512,128]{1,0:T(8,128)S(1)} %bitcast.15, f32[64,128]{1,0:T(8,128)S(1)} %get-tuple-element.19.seen_ref, f32[64,128]{1,0:T(8,128)S(1)} %get-tuple-element.20.noise_ref), custom_call_target="tpu_custom_call" | custom-call | tf_op jit(solution)/shard_map/pallas_call | solution.py:282
  142.5 11.3 %all_to_all.51 = f32[32,8,128]{2,1,0:T(8,128)S(1)} all-to-all(f32[32,8,128]{2,1,0:T(8,128)S(1)} %broadcast_in_dim.4), channel_id=1, replica_groups=mesh['slab'=8,'pencil'=32] {'pencil'}, dimensions={0} | all-to-all | bytes 262144 | tf_op jit(solution)/shard_map/all_to_all | solution.py:290
  153.9 9.2 %all_to_all.52.sums_ref = f32[8,8,128]{2,1,0:T(8,128)S(1)} all-to-all(f32[8,8,128]{2,1,0:T(8,128)S(1)} %broadcast_in_dim.5), channel_id=1, replica_groups=mesh['slab'=8,'pencil'=32] {'slab'}, dimensions={0} | all-to-all | bytes 65536 | tf_op jit(solution)/shard_map/all_to_all | solution.py:290
  163.1 3.5 %shard_map.103 = (f32[512,128]{1,0:T(8,128)}, f32[64,128]{1,0:T(8,128)}) custom-call(f32[8,8,128]{2,1,0:T(8,128)S(1)} %all_to_all.52.sums_ref, f32[512,128]{1,0:T(8,128)S(1)} %bitcast.16, f32[512,128]{1,0:T(8,128)S(1)} %get-tuple-element.22.first_ref, f32[512,128]{1,0:T(8,128)S(1)} %get-tuple-element.23.second_ref), custom_call_target="tpu_custom_call" | custom-call | tf_op jit(solution)/shard_map/pallas_call | solution.py:282
  (11 shorter events, 0.1 us)
Async XLA Ops:
  0.6 1.0 copy-start.2
  1.6 0.8 copy-start.6
  2.3 0.8 copy-start.7
  3.1 0.8 copy-start.8
  3.9 35.0 %copy-start.4 = (bf16[2,128,128]{2,1,0:T(8,128)(2,1)S(1)}, bf16[2,128,128]{2,1,0:T(8,128)(2,1)}, u32[]{:S(2)}) copy-start(bf16[2,128,128]{2,1,0:T(8,128)(2,1)} %constant.10.clone.table_ref.forward_ref) | copy-start | bytes 196612
  38.9 19.4 %copy-start = (bf16[4,2,256,256]{3,2,1,0:T(8,128)(2,1)S(1)}, bf16[4,2,256,256]{3,2,1,0:T(8,128)(2,1)}, u32[]{:S(2)}) copy-start(bf16[4,2,256,256]{3,2,1,0:T(8,128)(2,1)} %constant.12.clone.y_ref) | copy-start | bytes 3145732
  40.0 18.3 %copy-start.1 = (bf16[2,2,256,256]{3,2,1,0:T(8,128)(2,1)S(1)}, bf16[2,2,256,256]{3,2,1,0:T(8,128)(2,1)}, u32[]{:S(2)}) copy-start(bf16[2,2,256,256]{3,2,1,0:T(8,128)(2,1)} %constant.13.clone.z_ref) | copy-start | bytes 1572868
  40.0 18.3 %all-to-all-start.1 = ((f32[32,16,128]{2,1,0:T(8,128)}), f32[32,16,128]{2,1,0:T(8,128)S(1)}, u32[]{:S(2)}, u32[]{:S(2)}) async-start(f32[32,16,128]{2,1,0:T(8,128)} %bitcast.3), calls=%async_computation.1 | async-start | bytes 524288 | tf_op jit(solution)/shard_map/all_to_all | solution.py:290
  49.5 0.7 collective-permute-start
  59.9 12.6 %copy-start.5 = (bf16[2,128,128]{2,1,0:T(8,128)(2,1)S(1)}, bf16[2,128,128]{2,1,0:T(8,128)(2,1)}, u32[]{:S(2)}) copy-start(bf16[2,128,128]{2,1,0:T(8,128)(2,1)} %constant.11.clone.inverse_ref) | copy-start | bytes 196612
  113.8 26.2 %copy-start.3 = (f32[8,16,4,128]{3,2,1,0:T(4,128)S(1)}, f32[8,16,4,128]{3,2,1,0:T(4,128)}, u32[]{:S(2)}) copy-start(f32[8,16,4,128]{3,2,1,0:T(4,128)} %param.8) | copy-start | bytes 786436

commit v3 on v2

--- a/solution.py
+++ b/solution.py
@@ -7,6 +7,7 @@
 from jax.experimental import pallas as pl
 from jax.experimental.pallas import tpu as pltpu
 from jax.sharding import PartitionSpec as P
+
 
 GRID = 128
 CELLS = GRID**3
@@ -56,13 +57,10 @@
     ).reshape(-1)
     forward_y = forward[:, order]
     inverse_y = inverse[order, :]
-    is_real = (order < GRID)[None, :]
-    real_y = np.where(is_real, forward_y, 0.0)
-    imag_y = np.where(is_real, 0.0, np.block([[cosine, cosine], [-sine, -sine]])[:, order])
     return (
         split_table(forward_x),
         split_table(inverse_x),
-        np.stack([split_table(t) for t in (real_y, imag_y, forward_y, inverse_y)]),
+        np.stack([split_table(t) for t in (forward_y, inverse_y)]),
         np.stack([split_table(t) for t in (forward.T, inverse.T)]),
     )
 
@@ -99,30 +97,31 @@
         forward_x_lines(lines_of(staged_ref, line), line, table_ref, out_ref)
 
 
-def spectrum_of(in_ref, slot, y_ref, z_ref, kind):
-    block = in_ref[:, slot * 2 * LINES : (slot + 1) * 2 * LINES, :].reshape(2 * GRID, GRID)
-    rows = product(pair(y_ref, kind), halves(block), NN)
+def spectrum_of(block, y_ref, z_ref):
+    rows = product(pair(y_ref, 0), halves(block), NN)
     rows = jnp.concatenate((rows[:GRID], rows[GRID:]), axis=1)
-    waves = product(halves(rows), pair(z_ref, 0), NN)
-    return waves[:, :GRID], waves[:, GRID:]
+    return product(halves(rows), pair(z_ref, 0), NN)
+
+
+def slot_of(in_ref, slot):
+    return in_ref[:, slot * 2 * LINES : (slot + 1) * 2 * LINES, :].reshape(2 * GRID, GRID)
 
 
 def weighted_slots(in_ref, weights, y_ref, z_ref):
-    real_weight, imag_weight, other_weight = weights
-    real_re, real_im = spectrum_of(in_ref, 0, y_ref, z_ref, 0)
-    imag_re, imag_im = spectrum_of(in_ref, 0, y_ref, z_ref, 1)
-    other_re, other_im = spectrum_of(in_ref, 1, y_ref, z_ref, 2)
-    return (
-        (
-            real_weight * real_re - imag_weight * imag_im,
-            real_weight * real_im + imag_weight * imag_re,
-        ),
-        (other_weight * other_re, other_weight * other_im),
-    )
+    real_weight, imag_weight, other_weight = [
+        jnp.concatenate((weight, weight), axis=1) for weight in weights
+    ]
+    block = slot_of(in_ref, 0)
+    rows = lax.broadcasted_iota(jnp.int32, block.shape, 0)
+    is_real = rows % (2 * LINES) < LINES
+    real = spectrum_of(jnp.where(is_real, block, 0.0), y_ref, z_ref)
+    imag = spectrum_of(jnp.where(is_real, 0.0, block), y_ref, z_ref)
+    other = spectrum_of(slot_of(in_ref, 1), y_ref, z_ref)
+    return real_weight * real + imag_weight * imag, other_weight * other
 
 
 def plane_of(staged_ref, plane):
-    start = 3 * ROWS + DEPTH * plane
+    start = ROWS + DEPTH * plane
     return staged_ref[:, start : start + DEPTH, :].reshape(GRID, GRID)
 
 
@@ -135,22 +134,32 @@
 
 def middle_kernel(in_ref, staged_ref, edge_ref, y_ref, z_ref, out_ref):
     slots = weighted_slots(in_ref, eigen_planes(staged_ref, edge_ref)[1], y_ref, z_ref)
-    for slot, (real, imag) in enumerate(slots):
-        waves = jnp.concatenate((real, imag), axis=1)
+    for slot, waves in enumerate(slots):
         rows = product(halves(waves), pair(z_ref, 1), NN)
         rows = jnp.concatenate((rows[:, :GRID], rows[:, GRID:]), axis=0)
-        block = product(pair(y_ref, 3), halves(rows), NN)
+        block = product(pair(y_ref, 1), halves(rows), NN)
         out_ref[:, slot * 2 * LINES : (slot + 1) * 2 * LINES, :] = block.reshape(
             PENCILS, 2 * LINES, GRID
         )
 
 
-def back_kernel(in_ref, staged_ref, last_ref, inverse_ref, forward_ref, field_ref, out_ref):
+def neighbour(step):
+    return lax.rem(lax.axis_index("slab") + (SLABS + step), SLABS)
+
+
+def first_back_kernel(in_ref, last_ref, inverse_ref, forward_ref, *refs):
+    parts, (mask_ref, field_ref, out_ref) = refs[:SLABS], refs[SLABS:]
+    for step, part in enumerate(parts):
+        mask_ref[neighbour(-step)] = part[...]
+    back_kernel(in_ref, mask_ref, last_ref, inverse_ref, forward_ref, field_ref, out_ref)
+
+
+def back_kernel(in_ref, mask_ref, last_ref, inverse_ref, forward_ref, field_ref, out_ref):
     for line in range(LINES):
         waves = in_ref[pl.ds(line, GRID, stride=LINES), :]
         smooth = product(halves(waves), pair(inverse_ref), TN)
-        seen = lines_of(staged_ref, line, ROWS)
-        noise = lines_of(staged_ref, line, 2 * ROWS)
+        seen = lines_of(mask_ref, line)
+        noise = lines_of(mask_ref, line, ROWS)
         field = seen * smooth + noise * lines_of(last_ref, line)
         field_ref[:, pl.ds(line, DEPTH, stride=LINES), :] = field.reshape(SLABS, DEPTH, GRID)
         forward_x_lines(field, line, forward_ref, out_ref)
@@ -163,14 +172,17 @@
     factors = (single, single, share)
     weights = [jnp.sqrt(plane * factor) for plane, factor in zip(planes, factors)]
     slots = weighted_slots(in_ref, weights, y_ref, z_ref)
-    for index, values in enumerate((*slots[0], *slots[1])):
+    for index in range(4):
+        part = index % 2 * GRID
+        values = slots[index // 2][:, part : part + GRID]
         out_ref[:, index * DEPTH : (index + 1) * DEPTH, :] = values.reshape(SLABS, DEPTH, GRID)
-    out_ref[:, ROWS : 2 * ROWS, :] = first_ref[:, :ROWS, :]
-    out_ref[:, 2 * ROWS :, :] = second_ref[:, :ROWS, :]
-
-
-def gram_kernel(in_ref, base_ref, seen_ref, noise_ref, first_ref, second_ref, out_ref):
-    hidden = (1.0 - seen_ref[...]) * noise_ref[...]
+    out_ref[:, ROWS : 2 * ROWS, :] = first_ref[...]
+    out_ref[:, 2 * ROWS :, :] = second_ref[...]
+
+
+def gram_kernel(in_ref, base_ref, mask_ref, first_ref, second_ref, out_ref):
+    noise_ref = mask_ref.at[ROWS:, :]
+    hidden = (1.0 - mask_ref[:ROWS, :]) * noise_ref[...]
     hidden_twice = hidden * noise_ref[...]
     for column in range(COLUMNS):
         source = column * 3 * ROWS
@@ -250,24 +262,21 @@
     gradient_ref[...] = 0.5 * weighted
 
 
-def stage_kernel(base_ref, observed_ref, noise_ref, spectrum_ref, out_ref, seen_ref, shifted_ref):
+def stage_kernel(base_ref, observed_ref, noise_ref, spectrum_ref, out_ref, mask_ref):
     seen = observed_ref[...].astype(F32)
-    shifted = (noise_ref[...] - SHIFT) * (1.0 / WIDTH)
-    seen_ref[...] = seen
-    shifted_ref[...] = shifted
+    mask_ref[:ROWS, :] = seen
+    mask_ref[ROWS:, :] = (noise_ref[...] - SHIFT) * (1.0 / WIDTH)
     low = lax.axis_index("pencil") < PENCILS // 2
     first = jnp.where(low, spectrum_ref[0], spectrum_ref[1])
     second = jnp.where(low, spectrum_ref[1], spectrum_ref[2])
-    parts = (seen, shifted, first, second, spectrum_ref[0])
     for slab in range(SLABS):
         out_ref[slab, :ROWS, :] = base_ref[slab] * seen
-        start = ROWS
-        for part in parts:
-            out_ref[slab, start : start + part.shape[0], :] = part
-            start += part.shape[0]
-
-
-def call(kernel, *shapes, inputs=True, outputs=True):
+        for index, plane in enumerate((first, second, spectrum_ref[0])):
+            start = ROWS + index * DEPTH
+            out_ref[slab, start : start + DEPTH, :] = plane
+
+
+def call(kernel, *shapes, inputs=pltpu.VMEM, outputs=True):
     kind = pltpu.VMEM if outputs else jax.ShapeDtypeStruct
     outs = [kind(shape, F32) for shape in shapes]
     run = pl.pallas_call(
@@ -277,9 +286,7 @@
     )
 
     def placed(*values):
-        if inputs:
-            values = [pltpu.with_memory_space_constraint(value, pltpu.VMEM) for value in values]
-        return run(*values)
+        return run(*[pltpu.with_memory_space_constraint(value, inputs) for value in values])
 
     return placed
 
@@ -288,6 +295,11 @@
     shape = values.shape
     parts = values.reshape(count, -1, shape[-1])
     return lax.all_to_all(parts, axis, 0, 0, tiled=True)
+
+
+def shifted(values, step):
+    ring = [(slab, (slab + step) % SLABS) for slab in range(SLABS)]
+    return lax.ppermute(values, "slab", ring)
 
 
 def local(right_sides, spectrum, noise_var, observed):
@@ -295,8 +307,9 @@
     flat = (BLOCK, GRID)
     cube = (SLABS, ROWS, GRID)
     square = (ROWS, GRID)
-    staged, seen, noise = call(
-        stage_kernel, (SLABS, 3 * ROWS + 3 * DEPTH, GRID), square, square, inputs=False
+    double = (2 * ROWS, GRID)
+    staged, mask = call(
+        stage_kernel, (SLABS, ROWS + 3 * DEPTH, GRID), double, inputs=pltpu.HBM
     )(
         right_sides.reshape(cube),
         observed.reshape(square),
@@ -304,27 +317,31 @@
         spectrum,
     )
     staged = exchange(staged, "slab", SLABS)
-    edge = staged[:, 3 * ROWS + 2 * DEPTH :, :].reshape(GRID, GRID)
+    edge = staged[:, ROWS + 2 * DEPTH :, :].reshape(GRID, GRID)
     edge = lax.ppermute(edge, "pencil", [(PENCILS // 2, 0)])
+    masks = [mask]
+    for step in range(1, SLABS):
+        masks.append(shifted(mask, step))
 
     sent = call(start_kernel, flat)(staged, forward_x)
-    fields = [staged]
-    for _ in range(2):
-        parts = exchange(sent, "pencil", PENCILS)
-        sent = call(middle_kernel, parts.shape)(parts, staged, edge, y_tables, z_tables)
-        parts = exchange(sent, "pencil", PENCILS).reshape(flat)
-        field, sent = call(back_kernel, cube, flat)(
-            parts, staged, fields[-1], inverse_x, forward_x
-        )
-        fields.append(field)
+    parts = exchange(sent, "pencil", PENCILS)
+    sent = call(middle_kernel, parts.shape)(parts, staged, edge, y_tables, z_tables)
+    parts = exchange(sent, "pencil", PENCILS).reshape(flat)
+    masks, field, sent = call(first_back_kernel, (SLABS, *double), cube, flat)(
+        parts, staged, inverse_x, forward_x, *masks
+    )
+    parts = exchange(sent, "pencil", PENCILS)
+    sent = call(middle_kernel, parts.shape)(parts, staged, edge, y_tables, z_tables)
+    parts = exchange(sent, "pencil", PENCILS).reshape(flat)
+    second, sent = call(back_kernel, cube, flat)(parts, masks, field, inverse_x, forward_x)
     parts = exchange(sent, "pencil", PENCILS)
     merged = call(energy_kernel, (SLABS, 3 * ROWS, GRID))(
-        parts, staged, edge, fields[1], fields[2], y_tables, z_tables
+        parts, staged, edge, field, second, y_tables, z_tables
     )
     merged = exchange(merged, "slab", SLABS).reshape(-1, GRID)
     base = right_sides.reshape(flat)
     first, second, sums = call(gram_kernel, flat, flat, (COLUMNS, GRID))(
-        merged, base, seen, noise
+        merged, base, mask
     )
     sums = exchange(jnp.broadcast_to(sums[None], (PENCILS, COLUMNS, GRID)), "pencil", PENCILS)
     sums = jnp.sum(sums, axis=0)

time: 167 us -> 171 us (1.024)
  blocking collectives: 132 us -> 113 us
  starting transfers between devices: 10.1 us -> 23.4 us
  waiting for transfers between devices: 8.18 us -> 19.3 us
  local copies, waits for them, and re-layouts: 3.29 us -> 0.07 us
    all_to_all x8 -> x7, blocking collectives: 132 us -> 113 us  [exchange(): return lax.all_to_all(parts, axis, 0, 0, tiled=True)]
    ppermute x0 -> x7, waiting for transfers between devices: none -> 11.1 us  [shifted(): return lax.ppermute(values, 'slab', ring)]
    ppermute x0 -> x7, starting transfers between devices: none -> 9.34 us  [shifted(): return lax.ppermute(values, 'slab', ring)]
    all_to_all x1 -> x2, starting transfers between devices: 9.46 us -> 13.4 us  [exchange(): return lax.all_to_all(parts, axis, 0, 0, tiled=True)]
    unnamed x18 -> x10, local copies, waits for them, and re-layouts: 3.24 us -> 0.02 us
    all_to_all x1 -> x2, waiting for transfers between devices: 8.18 us -> 8.18 us  [exchange(): return lax.all_to_all(parts, axis, 0, 0, tiled=True)]
  transfers between devices with their start and end apart: 2 -> 10, of which waited for: 1 -> 4; matrix products, arithmetic and copies ran while one was open for 0% -> 0% of each run, Pallas kernels for 0% -> 0%
where the time goes in v3:
time: 171 us
  blocking collectives  113 us (66%)
  starting transfers between devices  23.4 us (14%)
  waiting for transfers between devices  19.3 us (11%)
  Pallas kernels  14.3 us (8%)
    all_to_all x7, blocking collectives, exchange(): return lax.all_to_all(parts, axis, 0, 0, tiled=True)  113 us
    pallas_call x9, Pallas kernels, placed(): run(*[pltpu.with_memory_space_constraint(value, inputs) for value in valu...  14.3 us
    all_to_all x2, starting transfers between devices, exchange(): return lax.all_to_all(parts, axis, 0, 0, tiled=True)  13.4 us
    ppermute x7, waiting for transfers between devices, shifted(): return lax.ppermute(values, 'slab', ring)  11.1 us
    ppermute x7, starting transfers between devices, shifted(): return lax.ppermute(values, 'slab', ring)  9.34 us
    all_to_all x2, waiting for transfers between devices, exchange(): return lax.all_to_all(parts, axis, 0, 0, tiled=True)  8.18 us
  transfers between devices with their start and end apart: 10, of which 4 were waited for; matrix products, arithmetic and copies ran while one was open for 0% of the time, Pallas kernels for 0%

profile of v3, /device:TPU:1, one launch (start us, length us, event | category | flops | bytes accessed | tf_op | source)
XLA Modules:
  0.0 170.8 jit_solution(3246472616968445316)
XLA Ops:
  0.6 1.0 shard_map.95
  1.6 0.0 copy-start.3
  1.7 23.7 %all_to_all.45.staged_ref.last_ref = f32[8,112,128]{2,1,0:T(8,128)S(1)} all-to-all(f32[8,112,128]{2,1,0:T(8,128)S(1)} %get-tuple-element.14), channel_id=1, replica_groups=mesh['slab'=8,'pencil'=32] {'slab'}, dimensions={0} | all-to-all | bytes 917504 | tf_op jit(solution)/shard_map/all_to_all | solution.py:297
  25.4 1.1 shard_map.96
  26.5 9.5 %all-to-all-start.1 = ((f32[32,16,128]{2,1,0:T(8,128)}), f32[32,16,128]{2,1,0:T(8,128)S(1)}, u32[]{:S(2)}, u32[]{:S(2)}) async-start(f32[32,16,128]{2,1,0:T(8,128)} %bitcast.3), calls=%async_computation.1 | async-start | bytes 524288 | tf_op jit(solution)/shard_map/all_to_all | solution.py:297
  36.0 0.7 collective-permute-start
  36.6 8.2 %all-to-all-done.1.in_ref = f32[32,16,128]{2,1,0:T(8,128)S(1)} async-done(((f32[32,16,128]{2,1,0:T(8,128)}), f32[32,16,128]{2,1,0:T(8,128)S(1)}, u32[]{:S(2)}, u32[]{:S(2)}) %all-to-all-start.1) | async-done | bytes 262176 | tf_op jit(solution)/shard_map/all_to_all | solution.py:297
  44.8 2.2 %shard_map.97 = f32[32,16,128]{2,1,0:T(8,128)} custom-call(f32[32,16,128]{2,1,0:T(8,128)S(1)} %all-to-all-done.1.in_ref, f32[8,112,128]{2,1,0:T(8,128)S(1)} %all_to_all.45.staged_ref.last_ref, f32[128,128]{1,0:T(8,128)S(1)} %collective-permute-done.edge_ref, bf16[2,2,256,256]{3,2,1,0:T(8,128)(2,1)S(1)} %copy-done.1, bf16[2,2,256,256]{3,2,1,0:T(8,128)(2,1)S(1)} %copy-done), custom_call_target="tpu_custom_call" | custom-call | tf_op jit(solution)/shard_map/pallas_call | solution.py:289
  47.1 3.9 %all-to-all-start.2 = ((f32[32,16,128]{2,1,0:T(8,128)}), f32[32,16,128]{2,1,0:T(8,128)S(1)}, u32[]{:S(2)}, u32[]{:S(2)}) async-start(f32[32,16,128]{2,1,0:T(8,128)} %shard_map.97), calls=%async_computation.2 | async-start | bytes 524288 | tf_op jit(solution)/shard_map/all_to_all | solution.py:297
  51.0 0.1 collective-permute-start.7
  51.1 0.6 collective-permute-start.6
  51.6 2.6 %collective-permute-start.5 = (f32[128,128]{1,0:T(8,128)S(1)}, f32[128,128]{1,0:T(8,128)S(1)}, u32[]{:S(2)}, u32[]{:S(2)}) collective-permute-start(f32[128,128]{1,0:T(8,128)S(1)} %get-tuple-element.15.refs_0_.mask_ref), channel_id=1, source_target_pairs={{0,160},{32,192},{64,224},{96,0},{128,32},{160,64},{192,96},{224,1... | collective-permute-start | bytes 196616 | tf_op jit(solution)/shard_map/ppermute | solution.py:302
  54.2 2.5 %collective-permute-start.4 = (f32[128,128]{1,0:T(8,128)S(1)}, f32[128,128]{1,0:T(8,128)S(1)}, u32[]{:S(2)}, u32[]{:S(2)}) collective-permute-start(f32[128,128]{1,0:T(8,128)S(1)} %get-tuple-element.15.refs_0_.mask_ref), channel_id=1, source_target_pairs={{0,128},{32,160},{64,192},{96,224},{128,0},{160,32},{192,64},{224,... | collective-permute-start | bytes 196616 | tf_op jit(solution)/shard_map/ppermute | solution.py:302
  56.7 2.4 %collective-permute-start.3 = (f32[128,128]{1,0:T(8,128)S(1)}, f32[128,128]{1,0:T(8,128)S(1)}, u32[]{:S(2)}, u32[]{:S(2)}) collective-permute-start(f32[128,128]{1,0:T(8,128)S(1)} %get-tuple-element.15.refs_0_.mask_ref), channel_id=1, source_target_pairs={{0,96},{32,128},{64,160},{96,192},{128,224},{160,0},{192,32},{224,... | collective-permute-start | bytes 196616 | tf_op jit(solution)/shard_map/ppermute | solution.py:302
  59.1 1.2 collective-permute-start.2
  60.3 0.0 collective-permute-done.6.refs_6_
  60.3 0.9 collective-permute-done.4.refs_4_
  61.3 7.6 %collective-permute-done.3.refs_3_ = f32[128,128]{1,0:T(8,128)S(1)} collective-permute-done((f32[128,128]{1,0:T(8,128)S(1)}, f32[128,128]{1,0:T(8,128)S(1)}, u32[]{:S(2)}, u32[]{:S(2)}) %collective-permute-start.3) | collective-permute-done | bytes 65568 | tf_op jit(solution)/shard_map/ppermute | solution.py:302
  68.9 2.5 %collective-permute-done.1.refs_1_ = f32[128,128]{1,0:T(8,128)S(1)} collective-permute-done((f32[128,128]{1,0:T(8,128)S(1)}, f32[128,128]{1,0:T(8,128)S(1)}, u32[]{:S(2)}, u32[]{:S(2)}) %collective-permute-start.1) | collective-permute-done | bytes 65568 | tf_op jit(solution)/shard_map/ppermute | solution.py:302
  71.4 0.7 shard_map.98
  72.2 16.3 %all_to_all.46.in_ref = f32[32,16,128]{2,1,0:T(8,128)S(1)} all-to-all(f32[32,16,128]{2,1,0:T(8,128)S(1)} %bitcast.19), channel_id=1, replica_groups=mesh['slab'=8,'pencil'=32] {'pencil'}, dimensions={0} | all-to-all | bytes 524288 | tf_op jit(solution)/shard_map/all_to_all | solution.py:297
  88.5 1.5 shard_map.99
  90.0 12.4 %all_to_all.47 = f32[32,16,128]{2,1,0:T(8,128)S(1)} all-to-all(f32[32,16,128]{2,1,0:T(8,128)S(1)} %shard_map.99), channel_id=1, replica_groups=mesh['slab'=8,'pencil'=32] {'pencil'}, dimensions={0} | all-to-all | bytes 524288 | tf_op jit(solution)/shard_map/all_to_all | solution.py:297
  102.5 0.7 shard_map.100
  103.2 12.4 %all_to_all.48.in_ref = f32[32,16,128]{2,1,0:T(8,128)S(1)} all-to-all(f32[32,16,128]{2,1,0:T(8,128)S(1)} %bitcast.20), channel_id=1, replica_groups=mesh['slab'=8,'pencil'=32] {'pencil'}, dimensions={0} | all-to-all | bytes 524288 | tf_op jit(solution)/shard_map/all_to_all | solution.py:297
  115.7 1.0 shard_map.101
  116.7 0.0 copy-start.2
  116.7 27.4 %all_to_all.49 = f32[8,192,128]{2,1,0:T(8,128)S(1)} all-to-all(f32[8,192,128]{2,1,0:T(8,128)S(1)} %shard_map.101), channel_id=1, replica_groups=mesh['slab'=8,'pencil'=32] {'slab'}, dimensions={0} | all-to-all | bytes 1572864 | tf_op jit(solution)/shard_map/all_to_all | solution.py:297
  144.1 2.5 %shard_map.102 = (f32[512,128]{1,0:T(8,128)S(1)}, f32[512,128]{1,0:T(8,128)S(1)}, f32[8,128]{1,0:T(8,128)S(1)}) custom-call(f32[1536,128]{1,0:T(8,128)S(1)} %bitcast.13, f32[512,128]{1,0:T(8,128)S(1)} %bitcast.15, f32[128,128]{1,0:T(8,128)S(1)} %get-tuple-element.15.refs_0_.mask_ref), custom_call_target="tpu_custom_call" | custom-call | tf_op jit(solution)/shard_map/pallas_call | solution.py:289
  146.6 11.4 %all_to_all.50 = f32[32,8,128]{2,1,0:T(8,128)S(1)} all-to-all(f32[32,8,128]{2,1,0:T(8,128)S(1)} %broadcast_in_dim.4), channel_id=1, replica_groups=mesh['slab'=8,'pencil'=32] {'pencil'}, dimensions={0} | all-to-all | bytes 262144 | tf_op jit(solution)/shard_map/all_to_all | solution.py:297
  158.1 9.2 %all_to_all.51.sums_ref = f32[8,8,128]{2,1,0:T(8,128)S(1)} all-to-all(f32[8,8,128]{2,1,0:T(8,128)S(1)} %broadcast_in_dim.5), channel_id=1, replica_groups=mesh['slab'=8,'pencil'=32] {'slab'}, dimensions={0} | all-to-all | bytes 65536 | tf_op jit(solution)/shard_map/all_to_all | solution.py:297
  167.3 3.5 %shard_map.103 = (f32[512,128]{1,0:T(8,128)}, f32[64,128]{1,0:T(8,128)}) custom-call(f32[8,8,128]{2,1,0:T(8,128)S(1)} %all_to_all.51.sums_ref, f32[512,128]{1,0:T(8,128)S(1)} %bitcast.16, f32[512,128]{1,0:T(8,128)S(1)} %get-tuple-element.22.first_ref, f32[512,128]{1,0:T(8,128)S(1)} %get-tuple-element.23.second_ref), custom_call_target="tpu_custom_call" | custom-call | tf_op jit(solution)/shard_map/pallas_call | solution.py:289
  (18 shorter events, 0.1 us)
Async XLA Ops:
  1.6 23.8 %copy-start.3 = (bf16[2,128,128]{2,1,0:T(8,128)(2,1)S(1)}, bf16[2,128,128]{2,1,0:T(8,128)(2,1)}, u32[]{:S(2)}) copy-start(bf16[2,128,128]{2,1,0:T(8,128)(2,1)} %constant.10.clone.table_ref.forward_ref) | copy-start | bytes 196612
  25.4 19.4 %copy-start.1 = (bf16[2,2,256,256]{3,2,1,0:T(8,128)(2,1)S(1)}, bf16[2,2,256,256]{3,2,1,0:T(8,128)(2,1)}, u32[]{:S(2)}) copy-start(bf16[2,2,256,256]{3,2,1,0:T(8,128)(2,1)} %constant.12.clone.y_ref) | copy-start | bytes 1572868
  26.5 18.3 %copy-start = (bf16[2,2,256,256]{3,2,1,0:T(8,128)(2,1)S(1)}, bf16[2,2,256,256]{3,2,1,0:T(8,128)(2,1)}, u32[]{:S(2)}) copy-start(bf16[2,2,256,256]{3,2,1,0:T(8,128)(2,1)} %constant.13.clone.z_ref) | copy-start | bytes 1572868
  26.5 18.3 %all-to-all-start.1 = ((f32[32,16,128]{2,1,0:T(8,128)}), f32[32,16,128]{2,1,0:T(8,128)S(1)}, u32[]{:S(2)}, u32[]{:S(2)}) async-start(f32[32,16,128]{2,1,0:T(8,128)} %bitcast.3), calls=%async_computation.1 | async-start | bytes 524288 | tf_op jit(solution)/shard_map/all_to_all | solution.py:297
  36.0 0.7 collective-permute-start
  47.1 24.4 %copy-start.4 = (bf16[2,128,128]{2,1,0:T(8,128)(2,1)S(1)}, bf16[2,128,128]{2,1,0:T(8,128)(2,1)}, u32[]{:S(2)}) copy-start(bf16[2,128,128]{2,1,0:T(8,128)(2,1)} %constant.11.clone.inverse_ref) | copy-start | bytes 196612
  47.1 24.4 %all-to-all-start.2 = ((f32[32,16,128]{2,1,0:T(8,128)}), f32[32,16,128]{2,1,0:T(8,128)S(1)}, u32[]{:S(2)}, u32[]{:S(2)}) async-start(f32[32,16,128]{2,1,0:T(8,128)} %shard_map.97), calls=%async_computation.2 | async-start | bytes 524288 | tf_op jit(solution)/shard_map/all_to_all | solution.py:297
  51.0 8.1 %collective-permute-start.7 = (f32[128,128]{1,0:T(8,128)S(1)}, f32[128,128]{1,0:T(8,128)S(1)}, u32[]{:S(2)}, u32[]{:S(2)}) collective-permute-start(f32[128,128]{1,0:T(8,128)S(1)} %get-tuple-element.15.refs_0_.mask_ref), channel_id=1, source_target_pairs={{0,224},{32,0},{64,32},{96,64},{128,96},{160,128},{192,160},{224,1... | collective-permute-start | bytes 196616 | tf_op jit(solution)/shard_map/ppermute | solution.py:302
  51.1 9.3 %collective-permute-start.6 = (f32[128,128]{1,0:T(8,128)S(1)}, f32[128,128]{1,0:T(8,128)S(1)}, u32[]{:S(2)}, u32[]{:S(2)}) collective-permute-start(f32[128,128]{1,0:T(8,128)S(1)} %get-tuple-element.15.refs_0_.mask_ref), channel_id=1, source_target_pairs={{0,192},{32,224},{64,0},{96,32},{128,64},{160,96},{192,128},{224,1... | collective-permute-start | bytes 196616 | tf_op jit(solution)/shard_map/ppermute | solution.py:302
  51.6 8.7 %collective-permute-start.5 = (f32[128,128]{1,0:T(8,128)S(1)}, f32[128,128]{1,0:T(8,128)S(1)}, u32[]{:S(2)}, u32[]{:S(2)}) collective-permute-start(f32[128,128]{1,0:T(8,128)S(1)} %get-tuple-element.15.refs_0_.mask_ref), channel_id=1, source_target_pairs={{0,160},{32,192},{64,224},{96,0},{128,32},{160,64},{192,96},{224,1... | collective-permute-start | bytes 196616 | tf_op jit(solution)/shard_map/ppermute | solution.py:302
  54.2 7.1 %collective-permute-start.4 = (f32[128,128]{1,0:T(8,128)S(1)}, f32[128,128]{1,0:T(8,128)S(1)}, u32[]{:S(2)}, u32[]{:S(2)}) collective-permute-start(f32[128,128]{1,0:T(8,128)S(1)} %get-tuple-element.15.refs_0_.mask_ref), channel_id=1, source_target_pairs={{0,128},{32,160},{64,192},{96,224},{128,0},{160,32},{192,64},{224,... | collective-permute-start | bytes 196616 | tf_op jit(solution)/shard_map/ppermute | solution.py:302
  56.7 12.2 %collective-permute-start.3 = (f32[128,128]{1,0:T(8,128)S(1)}, f32[128,128]{1,0:T(8,128)S(1)}, u32[]{:S(2)}, u32[]{:S(2)}) collective-permute-start(f32[128,128]{1,0:T(8,128)S(1)} %get-tuple-element.15.refs_0_.mask_ref), channel_id=1, source_target_pairs={{0,96},{32,128},{64,160},{96,192},{128,224},{160,0},{192,32},{224,... | collective-permute-start | bytes 196616 | tf_op jit(solution)/shard_map/ppermute | solution.py:302
  59.1 9.8 %collective-permute-start.2 = (f32[128,128]{1,0:T(8,128)S(1)}, f32[128,128]{1,0:T(8,128)S(1)}, u32[]{:S(2)}, u32[]{:S(2)}) collective-permute-start(f32[128,128]{1,0:T(8,128)S(1)} %get-tuple-element.15.refs_0_.mask_ref), channel_id=1, source_target_pairs={{0,64},{32,96},{64,128},{96,160},{128,192},{160,224},{192,0},{224,... | collective-permute-start | bytes 196616 | tf_op jit(solution)/shard_map/ppermute | solution.py:302
  60.3 11.1 %collective-permute-start.1 = (f32[128,128]{1,0:T(8,128)S(1)}, f32[128,128]{1,0:T(8,128)S(1)}, u32[]{:S(2)}, u32[]{:S(2)}) collective-permute-start(f32[128,128]{1,0:T(8,128)S(1)} %get-tuple-element.15.refs_0_.mask_ref), channel_id=1, source_target_pairs={{0,32},{32,64},{64,96},{96,128},{128,160},{160,192},{192,224},{224... | collective-permute-start | bytes 196616 | tf_op jit(solution)/shard_map/ppermute | solution.py:302
  116.7 27.4 %copy-start.2 = (f32[8,16,4,128]{3,2,1,0:T(4,128)S(1)}, f32[8,16,4,128]{3,2,1,0:T(4,128)}, u32[]{:S(2)}) copy-start(f32[8,16,4,128]{3,2,1,0:T(4,128)} %param.8) | copy-start | bytes 786436

commit v4 on v3

--- a/solution.py
+++ b/solution.py
@@ -18,6 +18,7 @@
 DEPTH = GRID // SLABS
 ROWS = DEPTH * LINES
 BLOCK = PENCILS * 4 * LINES
+TARGETS = 4
 SHIFT = 6.0
 WIDTH = 8.0
 F32 = jnp.float32
@@ -202,17 +203,21 @@
         halves(jnp.concatenate(parts, axis=1)) for parts in (zeroth, first, second, scaled, waves)
     ]
     out_ref[...] = jnp.zeros_like(out_ref)
+
+    def stacked(*parts):
+        return [jnp.concatenate(half, axis=0) for half in zip(*parts)]
+
     pairs = (
-        (zeroth, zeroth),
-        (zeroth, first),
-        (first, first),
-        (first, second),
-        (second, second),
-        (second, scaled),
+        (zeroth, stacked(zeroth, first)),
+        (first, stacked(first, second)),
+        (second, stacked(second, scaled)),
         (waves, waves),
     )
-    for index, (left, right) in enumerate(pairs):
-        out_ref[:, index * COLUMNS : (index + 1) * COLUMNS] = product(left, right, NT)
+    start = 0
+    for left, right in pairs:
+        sums = product(left, right, NT)
+        out_ref[:, start : start + sums.shape[1]] = sums
+        start += sums.shape[1]
 
 
 def solve_kernel(
@@ -238,27 +243,37 @@
         blocks.append(jnp.where(lanes < size, operator, moved(degree - step)))
     system = jnp.concatenate(blocks, axis=0)
     rows = lax.broadcasted_iota(jnp.int32, (size, 1), 0)
-    for step in range(size):
-        pivot_row = system[step : step + 1, :]
-        pivot_row = pivot_row / pivot_row[:, step : step + 1]
-        reduced = system - system[:, step : step + 1] * pivot_row
-        system = jnp.where(rows == step, pivot_row, reduced)
+    for step in range(0, size, 2):
+        upper, lower = system[step : step + 1, :], system[step + 1 : step + 2, :]
+        left, right = [
+            jnp.broadcast_to(system[:, lane : lane + 1], system.shape) for lane in (step, step + 1)
+        ]
+        top_left, low_left = left[step : step + 1], left[step + 1 : step + 2]
+        top_right, low_right = right[step : step + 1], right[step + 1 : step + 2]
+        scale = 1.0 / (top_left * low_right - top_right * low_left)
+        new_upper = (low_right * upper - top_right * lower) * scale
+        new_lower = (top_left * lower - low_left * upper) * scale
+        reduced = system - left * new_upper - right * new_lower
+        system = jnp.where(rows == step, new_upper, jnp.where(rows == step + 1, new_lower, reduced))
     sources = (base_ref, first_ref, second_ref)
+    share = 1.0 / (COLUMNS - 1)
     weighted = jnp.zeros((ROWS, GRID), F32)
-    for target in range(COLUMNS):
-        total = jnp.zeros((ROWS, GRID), F32)
+    for group in range(0, COLUMNS, TARGETS):
+        totals = [jnp.zeros((ROWS, GRID), F32)] * TARGETS
         for index in range(size):
-            block = sources[index // COLUMNS]
-            column = index % COLUMNS
-            coefficient = system[index : index + 1, size + target : size + target + 1]
-            total = total + coefficient * block[column * ROWS : (column + 1) * ROWS, :]
-        rows_out = slice(target * ROWS, (target + 1) * ROWS)
-        solution_ref[rows_out, :] = total
-        if target == 0:
-            weighted = total * total
-        else:
-            share = 1.0 / (COLUMNS - 1)
-            weighted = weighted - share * (total * base_ref[rows_out, :])
+            start = index % COLUMNS * ROWS
+            block = sources[index // COLUMNS][start : start + ROWS, :]
+            for target in range(TARGETS):
+                lane = size + group + target
+                coefficient = system[index : index + 1, lane : lane + 1]
+                totals[target] = totals[target] + coefficient * block
+        for target, total in enumerate(totals, group):
+            rows_out = slice(target * ROWS, (target + 1) * ROWS)
+            solution_ref[rows_out, :] = total
+            if target:
+                weighted = weighted - share * (total * base_ref[rows_out, :])
+            else:
+                weighted = total * total
     gradient_ref[...] = 0.5 * weighted
 
 
@@ -346,7 +361,7 @@
     sums = exchange(jnp.broadcast_to(sums[None], (PENCILS, COLUMNS, GRID)), "pencil", PENCILS)
     sums = jnp.sum(sums, axis=0)
     sums = exchange(jnp.broadcast_to(sums[None], (SLABS, COLUMNS, GRID)), "slab", SLABS)
-    solution, gradient = call(solve_kernel, flat, (ROWS, GRID), outputs=False)(
+    solution, gradient = call(solve_kernel, flat, square, outputs=False)(
         sums, base, first, second
     )
     return solution.reshape(right_sides.shape), gradient.reshape(noise_var.shape)

time: 171 us -> 170 us (level)
  no operation moved by 1% of the time
where the time goes in v4:
time: 170 us; the launch traced here: 169 us
  blocking collectives  113 us (66%)
  starting transfers between devices  23.4 us (14%)
  waiting for transfers between devices  19.3 us (11%)
  Pallas kernels  12.8 us (8%)
    all_to_all x7, blocking collectives, exchange(): return lax.all_to_all(parts, axis, 0, 0, tiled=True)  113 us
    all_to_all x2, starting transfers between devices, exchange(): return lax.all_to_all(parts, axis, 0, 0, tiled=True)  13.4 us
    pallas_call x9, Pallas kernels, placed(): run(*[pltpu.with_memory_space_constraint(value, inputs) for value in valu...  12.8 us
    ppermute x7, waiting for transfers between devices, shifted(): return lax.ppermute(values, 'slab', ring)  11.1 us
    ppermute x7, starting transfers between devices, shifted(): return lax.ppermute(values, 'slab', ring)  9.34 us
    all_to_all x2, waiting for transfers between devices, exchange(): return lax.all_to_all(parts, axis, 0, 0, tiled=True)  8.18 us
  transfers between devices with their start and end apart: 10, of which 4 were waited for; matrix products, arithmetic and copies ran while one was open for 0% of the time, Pallas kernels for 0%

profile of v4, /device:TPU:1, one launch (start us, length us, event | category | flops | bytes accessed | tf_op | source)
XLA Modules:
  0.0 169.3 jit_solution(2383878914597589309)
XLA Ops:
  0.6 1.0 shard_map.95
  1.6 0.0 copy-start.3
  1.7 23.7 %all_to_all.45.staged_ref.last_ref = f32[8,112,128]{2,1,0:T(8,128)S(1)} all-to-all(f32[8,112,128]{2,1,0:T(8,128)S(1)} %get-tuple-element.14), channel_id=1, replica_groups=mesh['slab'=8,'pencil'=32] {'slab'}, dimensions={0} | all-to-all | bytes 917504 | tf_op jit(solution)/shard_map/all_to_all | solution.py:312
  25.4 1.1 shard_map.96
  26.5 9.5 %all-to-all-start.1 = ((f32[32,16,128]{2,1,0:T(8,128)}), f32[32,16,128]{2,1,0:T(8,128)S(1)}, u32[]{:S(2)}, u32[]{:S(2)}) async-start(f32[32,16,128]{2,1,0:T(8,128)} %bitcast.3), calls=%async_computation.1 | async-start | bytes 524288 | tf_op jit(solution)/shard_map/all_to_all | solution.py:312
  36.0 0.7 collective-permute-start
  36.6 8.2 %all-to-all-done.1.in_ref = f32[32,16,128]{2,1,0:T(8,128)S(1)} async-done(((f32[32,16,128]{2,1,0:T(8,128)}), f32[32,16,128]{2,1,0:T(8,128)S(1)}, u32[]{:S(2)}, u32[]{:S(2)}) %all-to-all-start.1) | async-done | bytes 262176 | tf_op jit(solution)/shard_map/all_to_all | solution.py:312
  44.8 2.2 %shard_map.97 = f32[32,16,128]{2,1,0:T(8,128)} custom-call(f32[32,16,128]{2,1,0:T(8,128)S(1)} %all-to-all-done.1.in_ref, f32[8,112,128]{2,1,0:T(8,128)S(1)} %all_to_all.45.staged_ref.last_ref, f32[128,128]{1,0:T(8,128)S(1)} %collective-permute-done.edge_ref, bf16[2,2,256,256]{3,2,1,0:T(8,128)(2,1)S(1)} %copy-done.1, bf16[2,2,256,256]{3,2,1,0:T(8,128)(2,1)S(1)} %copy-done), custom_call_target="tpu_custom_call" | custom-call | tf_op jit(solution)/shard_map/pallas_call | solution.py:304
  47.1 3.9 %all-to-all-start.2 = ((f32[32,16,128]{2,1,0:T(8,128)}), f32[32,16,128]{2,1,0:T(8,128)S(1)}, u32[]{:S(2)}, u32[]{:S(2)}) async-start(f32[32,16,128]{2,1,0:T(8,128)} %shard_map.97), calls=%async_computation.2 | async-start | bytes 524288 | tf_op jit(solution)/shard_map/all_to_all | solution.py:312
  51.0 0.1 collective-permute-start.7
  51.1 0.6 collective-permute-start.6
  51.6 2.6 %collective-permute-start.5 = (f32[128,128]{1,0:T(8,128)S(1)}, f32[128,128]{1,0:T(8,128)S(1)}, u32[]{:S(2)}, u32[]{:S(2)}) collective-permute-start(f32[128,128]{1,0:T(8,128)S(1)} %get-tuple-element.15.refs_0_.mask_ref), channel_id=1, source_target_pairs={{0,160},{32,192},{64,224},{96,0},{128,32},{160,64},{192,96},{224,1... | collective-permute-start | bytes 196616 | tf_op jit(solution)/shard_map/ppermute | solution.py:317
  54.2 2.5 %collective-permute-start.4 = (f32[128,128]{1,0:T(8,128)S(1)}, f32[128,128]{1,0:T(8,128)S(1)}, u32[]{:S(2)}, u32[]{:S(2)}) collective-permute-start(f32[128,128]{1,0:T(8,128)S(1)} %get-tuple-element.15.refs_0_.mask_ref), channel_id=1, source_target_pairs={{0,128},{32,160},{64,192},{96,224},{128,0},{160,32},{192,64},{224,... | collective-permute-start | bytes 196616 | tf_op jit(solution)/shard_map/ppermute | solution.py:317
  56.7 2.4 %collective-permute-start.3 = (f32[128,128]{1,0:T(8,128)S(1)}, f32[128,128]{1,0:T(8,128)S(1)}, u32[]{:S(2)}, u32[]{:S(2)}) collective-permute-start(f32[128,128]{1,0:T(8,128)S(1)} %get-tuple-element.15.refs_0_.mask_ref), channel_id=1, source_target_pairs={{0,96},{32,128},{64,160},{96,192},{128,224},{160,0},{192,32},{224,... | collective-permute-start | bytes 196616 | tf_op jit(solution)/shard_map/ppermute | solution.py:317
  59.1 1.2 collective-permute-start.2
  60.3 0.0 collective-permute-done.6.refs_6_
  60.3 0.9 collective-permute-done.4.refs_4_
  61.3 7.6 %collective-permute-done.3.refs_3_ = f32[128,128]{1,0:T(8,128)S(1)} collective-permute-done((f32[128,128]{1,0:T(8,128)S(1)}, f32[128,128]{1,0:T(8,128)S(1)}, u32[]{:S(2)}, u32[]{:S(2)}) %collective-permute-start.3) | collective-permute-done | bytes 65568 | tf_op jit(solution)/shard_map/ppermute | solution.py:317
  68.9 2.5 %collective-permute-done.1.refs_1_ = f32[128,128]{1,0:T(8,128)S(1)} collective-permute-done((f32[128,128]{1,0:T(8,128)S(1)}, f32[128,128]{1,0:T(8,128)S(1)}, u32[]{:S(2)}, u32[]{:S(2)}) %collective-permute-start.1) | collective-permute-done | bytes 65568 | tf_op jit(solution)/shard_map/ppermute | solution.py:317
  71.4 0.7 shard_map.98
  72.2 16.3 %all_to_all.46.in_ref = f32[32,16,128]{2,1,0:T(8,128)S(1)} all-to-all(f32[32,16,128]{2,1,0:T(8,128)S(1)} %bitcast.19), channel_id=1, replica_groups=mesh['slab'=8,'pencil'=32] {'pencil'}, dimensions={0} | all-to-all | bytes 524288 | tf_op jit(solution)/shard_map/all_to_all | solution.py:312
  88.5 1.5 shard_map.99
  90.0 12.4 %all_to_all.47 = f32[32,16,128]{2,1,0:T(8,128)S(1)} all-to-all(f32[32,16,128]{2,1,0:T(8,128)S(1)} %shard_map.99), channel_id=1, replica_groups=mesh['slab'=8,'pencil'=32] {'pencil'}, dimensions={0} | all-to-all | bytes 524288 | tf_op jit(solution)/shard_map/all_to_all | solution.py:312
  102.5 0.7 shard_map.100
  103.2 12.4 %all_to_all.48.in_ref = f32[32,16,128]{2,1,0:T(8,128)S(1)} all-to-all(f32[32,16,128]{2,1,0:T(8,128)S(1)} %bitcast.20), channel_id=1, replica_groups=mesh['slab'=8,'pencil'=32] {'pencil'}, dimensions={0} | all-to-all | bytes 524288 | tf_op jit(solution)/shard_map/all_to_all | solution.py:312
  115.7 1.0 shard_map.101
  116.7 0.0 copy-start.2
  116.7 27.4 %all_to_all.49 = f32[8,192,128]{2,1,0:T(8,128)S(1)} all-to-all(f32[8,192,128]{2,1,0:T(8,128)S(1)} %shard_map.101), channel_id=1, replica_groups=mesh['slab'=8,'pencil'=32] {'slab'}, dimensions={0} | all-to-all | bytes 1572864 | tf_op jit(solution)/shard_map/all_to_all | solution.py:312
  144.1 1.9 %shard_map.102 = (f32[512,128]{1,0:T(8,128)S(1)}, f32[512,128]{1,0:T(8,128)S(1)}, f32[8,128]{1,0:T(8,128)S(1)}) custom-call(f32[1536,128]{1,0:T(8,128)S(1)} %bitcast.13, f32[512,128]{1,0:T(8,128)S(1)} %bitcast.15, f32[128,128]{1,0:T(8,128)S(1)} %get-tuple-element.15.refs_0_.mask_ref), custom_call_target="tpu_custom_call" | custom-call | tf_op jit(solution)/shard_map/pallas_call | solution.py:304
  146.0 11.4 %all_to_all.50 = f32[32,8,128]{2,1,0:T(8,128)S(1)} all-to-all(f32[32,8,128]{2,1,0:T(8,128)S(1)} %broadcast_in_dim.4), channel_id=1, replica_groups=mesh['slab'=8,'pencil'=32] {'pencil'}, dimensions={0} | all-to-all | bytes 262144 | tf_op jit(solution)/shard_map/all_to_all | solution.py:312
  157.4 9.2 %all_to_all.51.sums_ref = f32[8,8,128]{2,1,0:T(8,128)S(1)} all-to-all(f32[8,8,128]{2,1,0:T(8,128)S(1)} %broadcast_in_dim.5), channel_id=1, replica_groups=mesh['slab'=8,'pencil'=32] {'slab'}, dimensions={0} | all-to-all | bytes 65536 | tf_op jit(solution)/shard_map/all_to_all | solution.py:312
  166.7 2.6 %shard_map.103 = (f32[512,128]{1,0:T(8,128)}, f32[64,128]{1,0:T(8,128)}) custom-call(f32[8,8,128]{2,1,0:T(8,128)S(1)} %all_to_all.51.sums_ref, f32[512,128]{1,0:T(8,128)S(1)} %bitcast.16, f32[512,128]{1,0:T(8,128)S(1)} %get-tuple-element.22.first_ref, f32[512,128]{1,0:T(8,128)S(1)} %get-tuple-element.23.second_ref), custom_call_target="tpu_custom_call" | custom-call | tf_op jit(solution)/shard_map/pallas_call | solution.py:304
  (18 shorter events, 0.1 us)
Async XLA Ops:
  1.6 23.8 %copy-start.3 = (bf16[2,128,128]{2,1,0:T(8,128)(2,1)S(1)}, bf16[2,128,128]{2,1,0:T(8,128)(2,1)}, u32[]{:S(2)}) copy-start(bf16[2,128,128]{2,1,0:T(8,128)(2,1)} %constant.10.clone.table_ref.forward_ref) | copy-start | bytes 196612
  25.4 19.4 %copy-start.1 = (bf16[2,2,256,256]{3,2,1,0:T(8,128)(2,1)S(1)}, bf16[2,2,256,256]{3,2,1,0:T(8,128)(2,1)}, u32[]{:S(2)}) copy-start(bf16[2,2,256,256]{3,2,1,0:T(8,128)(2,1)} %constant.12.clone.y_ref) | copy-start | bytes 1572868
  26.5 18.3 %copy-start = (bf16[2,2,256,256]{3,2,1,0:T(8,128)(2,1)S(1)}, bf16[2,2,256,256]{3,2,1,0:T(8,128)(2,1)}, u32[]{:S(2)}) copy-start(bf16[2,2,256,256]{3,2,1,0:T(8,128)(2,1)} %constant.13.clone.z_ref) | copy-start | bytes 1572868
  26.5 18.3 %all-to-all-start.1 = ((f32[32,16,128]{2,1,0:T(8,128)}), f32[32,16,128]{2,1,0:T(8,128)S(1)}, u32[]{:S(2)}, u32[]{:S(2)}) async-start(f32[32,16,128]{2,1,0:T(8,128)} %bitcast.3), calls=%async_computation.1 | async-start | bytes 524288 | tf_op jit(solution)/shard_map/all_to_all | solution.py:312
  36.0 0.7 collective-permute-start
  47.1 24.4 %copy-start.4 = (bf16[2,128,128]{2,1,0:T(8,128)(2,1)S(1)}, bf16[2,128,128]{2,1,0:T(8,128)(2,1)}, u32[]{:S(2)}) copy-start(bf16[2,128,128]{2,1,0:T(8,128)(2,1)} %constant.11.clone.inverse_ref) | copy-start | bytes 196612
  47.1 24.4 %all-to-all-start.2 = ((f32[32,16,128]{2,1,0:T(8,128)}), f32[32,16,128]{2,1,0:T(8,128)S(1)}, u32[]{:S(2)}, u32[]{:S(2)}) async-start(f32[32,16,128]{2,1,0:T(8,128)} %shard_map.97), calls=%async_computation.2 | async-start | bytes 524288 | tf_op jit(solution)/shard_map/all_to_all | solution.py:312
  51.0 8.1 %collective-permute-start.7 = (f32[128,128]{1,0:T(8,128)S(1)}, f32[128,128]{1,0:T(8,128)S(1)}, u32[]{:S(2)}, u32[]{:S(2)}) collective-permute-start(f32[128,128]{1,0:T(8,128)S(1)} %get-tuple-element.15.refs_0_.mask_ref), channel_id=1, source_target_pairs={{0,224},{32,0},{64,32},{96,64},{128,96},{160,128},{192,160},{224,1... | collective-permute-start | bytes 196616 | tf_op jit(solution)/shard_map/ppermute | solution.py:317
  51.1 9.3 %collective-permute-start.6 = (f32[128,128]{1,0:T(8,128)S(1)}, f32[128,128]{1,0:T(8,128)S(1)}, u32[]{:S(2)}, u32[]{:S(2)}) collective-permute-start(f32[128,128]{1,0:T(8,128)S(1)} %get-tuple-element.15.refs_0_.mask_ref), channel_id=1, source_target_pairs={{0,192},{32,224},{64,0},{96,32},{128,64},{160,96},{192,128},{224,1... | collective-permute-start | bytes 196616 | tf_op jit(solution)/shard_map/ppermute | solution.py:317
  51.6 8.7 %collective-permute-start.5 = (f32[128,128]{1,0:T(8,128)S(1)}, f32[128,128]{1,0:T(8,128)S(1)}, u32[]{:S(2)}, u32[]{:S(2)}) collective-permute-start(f32[128,128]{1,0:T(8,128)S(1)} %get-tuple-element.15.refs_0_.mask_ref), channel_id=1, source_target_pairs={{0,160},{32,192},{64,224},{96,0},{128,32},{160,64},{192,96},{224,1... | collective-permute-start | bytes 196616 | tf_op jit(solution)/shard_map/ppermute | solution.py:317
  54.2 7.1 %collective-permute-start.4 = (f32[128,128]{1,0:T(8,128)S(1)}, f32[128,128]{1,0:T(8,128)S(1)}, u32[]{:S(2)}, u32[]{:S(2)}) collective-permute-start(f32[128,128]{1,0:T(8,128)S(1)} %get-tuple-element.15.refs_0_.mask_ref), channel_id=1, source_target_pairs={{0,128},{32,160},{64,192},{96,224},{128,0},{160,32},{192,64},{224,... | collective-permute-start | bytes 196616 | tf_op jit(solution)/shard_map/ppermute | solution.py:317
  56.7 12.2 %collective-permute-start.3 = (f32[128,128]{1,0:T(8,128)S(1)}, f32[128,128]{1,0:T(8,128)S(1)}, u32[]{:S(2)}, u32[]{:S(2)}) collective-permute-start(f32[128,128]{1,0:T(8,128)S(1)} %get-tuple-element.15.refs_0_.mask_ref), channel_id=1, source_target_pairs={{0,96},{32,128},{64,160},{96,192},{128,224},{160,0},{192,32},{224,... | collective-permute-start | bytes 196616 | tf_op jit(solution)/shard_map/ppermute | solution.py:317
  59.1 9.8 %collective-permute-start.2 = (f32[128,128]{1,0:T(8,128)S(1)}, f32[128,128]{1,0:T(8,128)S(1)}, u32[]{:S(2)}, u32[]{:S(2)}) collective-permute-start(f32[128,128]{1,0:T(8,128)S(1)} %get-tuple-element.15.refs_0_.mask_ref), channel_id=1, source_target_pairs={{0,64},{32,96},{64,128},{96,160},{128,192},{160,224},{192,0},{224,... | collective-permute-start | bytes 196616 | tf_op jit(solution)/shard_map/ppermute | solution.py:317
  60.3 11.1 %collective-permute-start.1 = (f32[128,128]{1,0:T(8,128)S(1)}, f32[128,128]{1,0:T(8,128)S(1)}, u32[]{:S(2)}, u32[]{:S(2)}) collective-permute-start(f32[128,128]{1,0:T(8,128)S(1)} %get-tuple-element.15.refs_0_.mask_ref), channel_id=1, source_target_pairs={{0,32},{32,64},{64,96},{96,128},{128,160},{160,192},{192,224},{224... | collective-permute-start | bytes 196616 | tf_op jit(solution)/shard_map/ppermute | solution.py:317
  116.7 27.4 %copy-start.2 = (f32[8,16,4,128]{3,2,1,0:T(4,128)S(1)}, f32[8,16,4,128]{3,2,1,0:T(4,128)}, u32[]{:S(2)}) copy-start(f32[8,16,4,128]{3,2,1,0:T(4,128)} %param.8) | copy-start | bytes 786436

commit v5 on v4

--- a/solution.py
+++ b/solution.py
@@ -19,8 +19,9 @@
 ROWS = DEPTH * LINES
 BLOCK = PENCILS * 4 * LINES
 TARGETS = 4
-SHIFT = 6.0
 WIDTH = 8.0
+TILE = 8
+SMALLEST = 4e-7
 F32 = jnp.float32
 BF16 = jnp.bfloat16
 
@@ -81,6 +82,11 @@
     return dot(left[0], right[0]) + (dot(left[0], right[1]) + dot(left[1], right[0]))
 
 
+def full_product(left, right, dims):
+    dot = functools.partial(lax.dot_general, dimension_numbers=dims, preferred_element_type=F32)
+    return product(left, right, dims) + dot(left[1], right[1])
+
+
 def pair(ref, *index):
     return ref[(*index, 0)], ref[(*index, 1)]
 
@@ -144,23 +150,43 @@
         )
 
 
+def first_middle_kernel(in_ref, staged_ref, edge_ref, y_ref, z_ref, out_ref):
+    middle_kernel(in_ref, staged_ref, edge_ref, y_ref, z_ref, out_ref)
+    totals = jnp.sum(staged_ref[:, ROWS + 3 * DEPTH :, :], axis=0)
+    out_ref[:, 4 * LINES :, :] = jnp.broadcast_to(totals[None], (PENCILS, TILE, GRID))
+
+
 def neighbour(step):
     return lax.rem(lax.axis_index("slab") + (SLABS + step), SLABS)
 
 
 def first_back_kernel(in_ref, last_ref, inverse_ref, forward_ref, *refs):
-    parts, (mask_ref, field_ref, out_ref) = refs[:SLABS], refs[SLABS:]
+    parts, (mask_ref, shift_ref, field_ref, out_ref, flat_ref) = refs[:SLABS], refs[SLABS:]
     for step, part in enumerate(parts):
         mask_ref[neighbour(-step)] = part[...]
-    back_kernel(in_ref, mask_ref, last_ref, inverse_ref, forward_ref, field_ref, out_ref)
-
-
-def back_kernel(in_ref, mask_ref, last_ref, inverse_ref, forward_ref, field_ref, out_ref):
+    totals = jnp.sum(in_ref[:, 4 * LINES :, :], axis=0)
+    seen, noise, eigen = [
+        jnp.sum(totals[row : row + 1, :], axis=1, keepdims=True) * (1.0 / CELLS) for row in range(3)
+    ]
+    shift_ref[...] = jnp.broadcast_to(seen * eigen + noise, shift_ref.shape)
+    flat_ref[...] = in_ref[:, : 4 * LINES, :].reshape(BLOCK, GRID)
+    back_kernel(
+        flat_ref, mask_ref, shift_ref, last_ref, inverse_ref, forward_ref, field_ref, out_ref
+    )
+
+
+def shifted_noise(noise, shift_ref):
+    return (noise - shift_ref[0:1, :]) * (1.0 / WIDTH)
+
+
+def back_kernel(
+    in_ref, mask_ref, shift_ref, last_ref, inverse_ref, forward_ref, field_ref, out_ref
+):
     for line in range(LINES):
         waves = in_ref[pl.ds(line, GRID, stride=LINES), :]
         smooth = product(halves(waves), pair(inverse_ref), TN)
         seen = lines_of(mask_ref, line)
-        noise = lines_of(mask_ref, line, ROWS)
+        noise = shifted_noise(lines_of(mask_ref, line, ROWS), shift_ref)
         field = seen * smooth + noise * lines_of(last_ref, line)
         field_ref[:, pl.ds(line, DEPTH, stride=LINES), :] = field.reshape(SLABS, DEPTH, GRID)
         forward_x_lines(field, line, forward_ref, out_ref)
@@ -181,10 +207,10 @@
     out_ref[:, 2 * ROWS :, :] = second_ref[...]
 
 
-def gram_kernel(in_ref, base_ref, mask_ref, first_ref, second_ref, out_ref):
-    noise_ref = mask_ref.at[ROWS:, :]
-    hidden = (1.0 - mask_ref[:ROWS, :]) * noise_ref[...]
-    hidden_twice = hidden * noise_ref[...]
+def gram_kernel(in_ref, base_ref, mask_ref, shift_ref, first_ref, second_ref, out_ref):
+    noise = shifted_noise(mask_ref[ROWS:, :], shift_ref)
+    hidden = (1.0 - mask_ref[:ROWS, :]) * noise
+    hidden_twice = hidden * noise
     for column in range(COLUMNS):
         source = column * 3 * ROWS
         rows = slice(column * ROWS, (column + 1) * ROWS)
@@ -197,7 +223,7 @@
         zeroth.append(base_ref[pick, :])
         first.append(first_ref[pick, :])
         second.append(second_ref[pick, :])
-        scaled.append(second[-1] * noise_ref[row : row + 1, :])
+        scaled.append(second[-1] * noise[row : row + 1, :])
         waves.append(in_ref[pl.ds(row, COLUMNS, stride=3 * ROWS), :])
     zeroth, first, second, scaled, waves = [
         halves(jnp.concatenate(parts, axis=1)) for parts in (zeroth, first, second, scaled, waves)
@@ -215,13 +241,13 @@
     )
     start = 0
     for left, right in pairs:
-        sums = product(left, right, NT)
+        sums = full_product(left, right, NT)
         out_ref[:, start : start + sums.shape[1]] = sums
         start += sums.shape[1]
 
 
 def solve_kernel(
-    sums_ref, base_ref, first_ref, second_ref, solution_ref, gradient_ref
+    sums_ref, shift_ref, base_ref, first_ref, second_ref, solution_ref, gradient_ref
 ):
     lanes = lax.broadcasted_iota(jnp.int32, (COLUMNS, GRID), 1)
     moments = sums_ref[0]
@@ -237,12 +263,13 @@
     size = degree * COLUMNS
     blocks = []
     for step in range(degree):
-        operator = WIDTH * moved(GRID // COLUMNS - step - 1) + SHIFT * moved(
+        operator = WIDTH * moved(GRID // COLUMNS - step - 1) + shift_ref[...] * moved(
             (GRID // COLUMNS - step) % (GRID // COLUMNS)
         )
         blocks.append(jnp.where(lanes < size, operator, moved(degree - step)))
     system = jnp.concatenate(blocks, axis=0)
     rows = lax.broadcasted_iota(jnp.int32, (size, 1), 0)
+    given = system
     for step in range(0, size, 2):
         upper, lower = system[step : step + 1, :], system[step + 1 : step + 2, :]
         left, right = [
@@ -250,7 +277,11 @@
         ]
         top_left, low_left = left[step : step + 1], left[step + 1 : step + 2]
         top_right, low_right = right[step : step + 1], right[step + 1 : step + 2]
-        scale = 1.0 / (top_left * low_right - top_right * low_left)
+        area = top_left * low_right - top_right * low_left
+        top_limit = SMALLEST * given[step : step + 1, step : step + 1]
+        low_limit = SMALLEST * given[step + 1 : step + 2, step + 1 : step + 2]
+        apart = (top_left > top_limit) & (area > low_limit * top_left)
+        scale = jnp.where(apart, 1.0 / area, 0.0)
         new_upper = (low_right * upper - top_right * lower) * scale
         new_lower = (top_left * lower - low_left * upper) * scale
         reduced = system - left * new_upper - right * new_lower
@@ -280,23 +311,30 @@
 def stage_kernel(base_ref, observed_ref, noise_ref, spectrum_ref, out_ref, mask_ref):
     seen = observed_ref[...].astype(F32)
     mask_ref[:ROWS, :] = seen
-    mask_ref[ROWS:, :] = (noise_ref[...] - SHIFT) * (1.0 / WIDTH)
+    mask_ref[ROWS:, :] = noise_ref[...]
     low = lax.axis_index("pencil") < PENCILS // 2
     first = jnp.where(low, spectrum_ref[0], spectrum_ref[1])
     second = jnp.where(low, spectrum_ref[1], spectrum_ref[2])
+    totals = [
+        jnp.sum(values, axis=0, keepdims=True)
+        for values in (seen, noise_ref[...], spectrum_ref[...].reshape(-1, GRID))
+    ]
+    totals = jnp.concatenate((*totals, jnp.zeros((TILE - 3, GRID), F32)), axis=0)
     for slab in range(SLABS):
         out_ref[slab, :ROWS, :] = base_ref[slab] * seen
+        out_ref[slab, ROWS + 3 * DEPTH :, :] = totals
         for index, plane in enumerate((first, second, spectrum_ref[0])):
             start = ROWS + index * DEPTH
             out_ref[slab, start : start + DEPTH, :] = plane
 
 
-def call(kernel, *shapes, inputs=pltpu.VMEM, outputs=True):
+def call(kernel, *shapes, inputs=pltpu.VMEM, outputs=True, scratch=()):
     kind = pltpu.VMEM if outputs else jax.ShapeDtypeStruct
     outs = [kind(shape, F32) for shape in shapes]
     run = pl.pallas_call(
         kernel,
         out_shape=outs if len(outs) > 1 else outs[0],
+        scratch_shapes=scratch,
         compiler_params=pltpu.CompilerParams(vmem_limit_bytes=24 * 2**20),
     )
 
@@ -324,7 +362,7 @@
     square = (ROWS, GRID)
     double = (2 * ROWS, GRID)
     staged, mask = call(
-        stage_kernel, (SLABS, ROWS + 3 * DEPTH, GRID), double, inputs=pltpu.HBM
+        stage_kernel, (SLABS, ROWS + 3 * DEPTH + TILE, GRID), double, inputs=pltpu.HBM
     )(
         right_sides.reshape(cube),
         observed.reshape(square),
@@ -332,7 +370,8 @@
         spectrum,
     )
     staged = exchange(staged, "slab", SLABS)
-    edge = staged[:, ROWS + 2 * DEPTH :, :].reshape(GRID, GRID)
+    start = ROWS + 2 * DEPTH
+    edge = staged[:, start : start + DEPTH, :].reshape(GRID, GRID)
     edge = lax.ppermute(edge, "pencil", [(PENCILS // 2, 0)])
     masks = [mask]
     for step in range(1, SLABS):
@@ -340,15 +379,20 @@
 
     sent = call(start_kernel, flat)(staged, forward_x)
     parts = exchange(sent, "pencil", PENCILS)
-    sent = call(middle_kernel, parts.shape)(parts, staged, edge, y_tables, z_tables)
-    parts = exchange(sent, "pencil", PENCILS).reshape(flat)
-    masks, field, sent = call(first_back_kernel, (SLABS, *double), cube, flat)(
-        parts, staged, inverse_x, forward_x, *masks
-    )
+    sent = call(first_middle_kernel, (PENCILS, 4 * LINES + TILE, GRID))(
+        parts, staged, edge, y_tables, z_tables
+    )
+    parts = exchange(sent, "pencil", PENCILS)
+    tile = (TILE, GRID)
+    masks, shift, field, sent = call(
+        first_back_kernel, (SLABS, *double), tile, cube, flat, scratch=(pltpu.VMEM(flat, F32),)
+    )(parts, staged, inverse_x, forward_x, *masks)
     parts = exchange(sent, "pencil", PENCILS)
     sent = call(middle_kernel, parts.shape)(parts, staged, edge, y_tables, z_tables)
     parts = exchange(sent, "pencil", PENCILS).reshape(flat)
-    second, sent = call(back_kernel, cube, flat)(parts, masks, field, inverse_x, forward_x)
+    second, sent = call(back_kernel, cube, flat)(
+        parts, masks, shift, field, inverse_x, forward_x
+    )
     parts = exchange(sent, "pencil", PENCILS)
     merged = call(energy_kernel, (SLABS, 3 * ROWS, GRID))(
         parts, staged, edge, field, second, y_tables, z_tables
@@ -356,13 +400,13 @@
     merged = exchange(merged, "slab", SLABS).reshape(-1, GRID)
     base = right_sides.reshape(flat)
     first, second, sums = call(gram_kernel, flat, flat, (COLUMNS, GRID))(
-        merged, base, mask
+        merged, base, mask, shift
     )
     sums = exchange(jnp.broadcast_to(sums[None], (PENCILS, COLUMNS, GRID)), "pencil", PENCILS)
     sums = jnp.sum(sums, axis=0)
     sums = exchange(jnp.broadcast_to(sums[None], (SLABS, COLUMNS, GRID)), "slab", SLABS)
     solution, gradient = call(solve_kernel, flat, square, outputs=False)(
-        sums, base, first, second
+        sums, shift, base, first, second
     )
     return solution.reshape(right_sides.shape), gradient.reshape(noise_var.shape)
 

time: 170 us -> 171 us (level)
  no operation moved by 1% of the time
where the time goes in v5:
time: 171 us
  blocking collectives  114 us (67%)
  starting transfers between devices  23.4 us (14%)
  waiting for transfers between devices  19.3 us (11%)
  Pallas kernels  13.4 us (8%)
    all_to_all x7, blocking collectives, exchange(): return lax.all_to_all(parts, axis, 0, 0, tiled=True)  114 us
    all_to_all x2, starting transfers between devices, exchange(): return lax.all_to_all(parts, axis, 0, 0, tiled=True)  13.4 us
    pallas_call x9, Pallas kernels, placed(): run(*[pltpu.with_memory_space_constraint(value, inputs) for value in valu...  13.4 us
    ppermute x7, waiting for transfers between devices, shifted(): return lax.ppermute(values, 'slab', ring)  11.2 us
    ppermute x7, starting transfers between devices, shifted(): return lax.ppermute(values, 'slab', ring)  9.29 us
    all_to_all x2, waiting for transfers between devices, exchange(): return lax.all_to_all(parts, axis, 0, 0, tiled=True)  8.18 us
  transfers between devices with their start and end apart: 10, of which 4 were waited for; matrix products, arithmetic and copies ran while one was open for 0% of the time, Pallas kernels for 0%

profile of v5, /device:TPU:1, one launch (start us, length us, event | category | flops | bytes accessed | tf_op | source)
XLA Modules:
  0.0 170.5 jit_solution(10895701816202088739)
XLA Ops:
  0.6 1.0 shard_map.95
  1.6 0.0 copy-start.3
  1.7 24.4 %all_to_all.45.staged_ref.last_ref = f32[8,120,128]{2,1,0:T(8,128)S(1)} all-to-all(f32[8,120,128]{2,1,0:T(8,128)S(1)} %get-tuple-element.15), channel_id=1, replica_groups=mesh['slab'=8,'pencil'=32] {'slab'}, dimensions={0} | all-to-all | bytes 983040 | tf_op jit(solution)/shard_map/all_to_all | solution.py:350
  26.1 1.1 shard_map.96
  27.2 9.5 %all-to-all-start.1 = ((f32[32,16,128]{2,1,0:T(8,128)}), f32[32,16,128]{2,1,0:T(8,128)S(1)}, u32[]{:S(2)}, u32[]{:S(2)}) async-start(f32[32,16,128]{2,1,0:T(8,128)} %bitcast.3), calls=%async_computation.1 | async-start | bytes 524288 | tf_op jit(solution)/shard_map/all_to_all | solution.py:350
  36.7 0.7 collective-permute-start
  37.3 0.0 collective-permute-done.edge_ref
  37.4 8.2 %all-to-all-done.1.in_ref = f32[32,16,128]{2,1,0:T(8,128)S(1)} async-done(((f32[32,16,128]{2,1,0:T(8,128)}), f32[32,16,128]{2,1,0:T(8,128)S(1)}, u32[]{:S(2)}, u32[]{:S(2)}) %all-to-all-start.1) | async-done | bytes 262176 | tf_op jit(solution)/shard_map/all_to_all | solution.py:350
  45.5 2.3 %shard_map.97 = f32[32,24,128]{2,1,0:T(8,128)} custom-call(f32[32,16,128]{2,1,0:T(8,128)S(1)} %all-to-all-done.1.in_ref, f32[8,120,128]{2,1,0:T(8,128)S(1)} %all_to_all.45.staged_ref.last_ref, f32[128,128]{1,0:T(8,128)S(1)} %collective-permute-done.edge_ref, bf16[2,2,256,256]{3,2,1,0:T(8,128)(2,1)S(1)} %copy-done.1, bf16[2,2,256,256]{3,2,1,0:T(8,128)(2,1)S(1)} %copy-done), custom_call_target="tpu_custom_call" | custom-call | tf_op jit(solution)/shard_map/pallas_call | solution.py:342
  47.8 3.9 %all-to-all-start.2 = ((f32[32,24,128]{2,1,0:T(8,128)}), f32[32,24,128]{2,1,0:T(8,128)S(1)}, u32[]{:S(2)}, u32[]{:S(2)}) async-start(f32[32,24,128]{2,1,0:T(8,128)} %shard_map.97), calls=%async_computation.2 | async-start | bytes 786432 | tf_op jit(solution)/shard_map/all_to_all | solution.py:350
  51.7 0.1 collective-permute-start.7
  51.8 0.6 collective-permute-start.6
  52.4 2.6 %collective-permute-start.5 = (f32[128,128]{1,0:T(8,128)S(1)}, f32[128,128]{1,0:T(8,128)S(1)}, u32[]{:S(2)}, u32[]{:S(2)}) collective-permute-start(f32[128,128]{1,0:T(8,128)S(1)} %get-tuple-element.16.refs_0_.mask_ref), channel_id=1, source_target_pairs={{0,160},{32,192},{64,224},{96,0},{128,32},{160,64},{192,96},{224,1... | collective-permute-start | bytes 196616 | tf_op jit(solution)/shard_map/ppermute | solution.py:355
  55.0 2.5 %collective-permute-start.4 = (f32[128,128]{1,0:T(8,128)S(1)}, f32[128,128]{1,0:T(8,128)S(1)}, u32[]{:S(2)}, u32[]{:S(2)}) collective-permute-start(f32[128,128]{1,0:T(8,128)S(1)} %get-tuple-element.16.refs_0_.mask_ref), channel_id=1, source_target_pairs={{0,128},{32,160},{64,192},{96,224},{128,0},{160,32},{192,64},{224,... | collective-permute-start | bytes 196616 | tf_op jit(solution)/shard_map/ppermute | solution.py:355
  57.5 2.4 %collective-permute-start.3 = (f32[128,128]{1,0:T(8,128)S(1)}, f32[128,128]{1,0:T(8,128)S(1)}, u32[]{:S(2)}, u32[]{:S(2)}) collective-permute-start(f32[128,128]{1,0:T(8,128)S(1)} %get-tuple-element.16.refs_0_.mask_ref), channel_id=1, source_target_pairs={{0,96},{32,128},{64,160},{96,192},{128,224},{160,0},{192,32},{224,... | collective-permute-start | bytes 196616 | tf_op jit(solution)/shard_map/ppermute | solution.py:355
  59.8 1.2 collective-permute-start.2
  61.1 1.0 collective-permute-done.4.refs_4_
  62.0 7.5 %collective-permute-done.3.refs_3_ = f32[128,128]{1,0:T(8,128)S(1)} collective-permute-done((f32[128,128]{1,0:T(8,128)S(1)}, f32[128,128]{1,0:T(8,128)S(1)}, u32[]{:S(2)}, u32[]{:S(2)}) %collective-permute-start.3) | collective-permute-done | bytes 65568 | tf_op jit(solution)/shard_map/ppermute | solution.py:355
  69.5 2.7 %collective-permute-done.1.refs_1_ = f32[128,128]{1,0:T(8,128)S(1)} collective-permute-done((f32[128,128]{1,0:T(8,128)S(1)}, f32[128,128]{1,0:T(8,128)S(1)}, u32[]{:S(2)}, u32[]{:S(2)}) %collective-permute-start.1) | collective-permute-done | bytes 65568 | tf_op jit(solution)/shard_map/ppermute | solution.py:355
  72.2 0.8 shard_map.98
  73.0 16.3 %all_to_all.46.in_ref = f32[32,16,128]{2,1,0:T(8,128)S(1)} all-to-all(f32[32,16,128]{2,1,0:T(8,128)S(1)} %bitcast.17), channel_id=1, replica_groups=mesh['slab'=8,'pencil'=32] {'pencil'}, dimensions={0} | all-to-all | bytes 524288 | tf_op jit(solution)/shard_map/all_to_all | solution.py:350
  89.3 1.5 shard_map.99
  90.8 12.4 %all_to_all.47 = f32[32,16,128]{2,1,0:T(8,128)S(1)} all-to-all(f32[32,16,128]{2,1,0:T(8,128)S(1)} %shard_map.99), channel_id=1, replica_groups=mesh['slab'=8,'pencil'=32] {'pencil'}, dimensions={0} | all-to-all | bytes 524288 | tf_op jit(solution)/shard_map/all_to_all | solution.py:350
  103.3 0.7 shard_map.100
  104.0 12.4 %all_to_all.48.in_ref = f32[32,16,128]{2,1,0:T(8,128)S(1)} all-to-all(f32[32,16,128]{2,1,0:T(8,128)S(1)} %bitcast.18), channel_id=1, replica_groups=mesh['slab'=8,'pencil'=32] {'pencil'}, dimensions={0} | all-to-all | bytes 524288 | tf_op jit(solution)/shard_map/all_to_all | solution.py:350
  116.4 1.0 shard_map.101
  117.5 0.0 copy-start.2
  117.5 27.4 %all_to_all.49 = f32[8,192,128]{2,1,0:T(8,128)S(1)} all-to-all(f32[8,192,128]{2,1,0:T(8,128)S(1)} %shard_map.101), channel_id=1, replica_groups=mesh['slab'=8,'pencil'=32] {'slab'}, dimensions={0} | all-to-all | bytes 1572864 | tf_op jit(solution)/shard_map/all_to_all | solution.py:350
  144.8 2.3 %shard_map.102 = (f32[512,128]{1,0:T(8,128)S(1)}, f32[512,128]{1,0:T(8,128)S(1)}, f32[8,128]{1,0:T(8,128)S(1)}) custom-call(f32[1536,128]{1,0:T(8,128)S(1)} %bitcast.12, f32[512,128]{1,0:T(8,128)S(1)} %bitcast.14, f32[128,128]{1,0:T(8,128)S(1)} %get-tuple-element.16.refs_0_.mask_ref, f32[8,128]{1,0:T(8,128)S(1)} %get-tuple-element.19.shift_ref), custom_call_target="tpu_custom_call" | custom-call | tf_op jit(solution)/shard_map/pallas_call | solution.py:342
  147.2 11.4 %all_to_all.50 = f32[32,8,128]{2,1,0:T(8,128)S(1)} all-to-all(f32[32,8,128]{2,1,0:T(8,128)S(1)} %broadcast_in_dim.4), channel_id=1, replica_groups=mesh['slab'=8,'pencil'=32] {'pencil'}, dimensions={0} | all-to-all | bytes 262144 | tf_op jit(solution)/shard_map/all_to_all | solution.py:350
  158.7 9.2 %all_to_all.51.sums_ref = f32[8,8,128]{2,1,0:T(8,128)S(1)} all-to-all(f32[8,8,128]{2,1,0:T(8,128)S(1)} %broadcast_in_dim.5), channel_id=1, replica_groups=mesh['slab'=8,'pencil'=32] {'slab'}, dimensions={0} | all-to-all | bytes 65536 | tf_op jit(solution)/shard_map/all_to_all | solution.py:350
  167.9 2.6 %shard_map.103 = (f32[512,128]{1,0:T(8,128)}, f32[64,128]{1,0:T(8,128)}) custom-call(f32[8,8,128]{2,1,0:T(8,128)S(1)} %all_to_all.51.sums_ref, f32[8,128]{1,0:T(8,128)S(1)} %get-tuple-element.19.shift_ref, f32[512,128]{1,0:T(8,128)S(1)} %bitcast.15, f32[512,128]{1,0:T(8,128)S(1)} %get-tuple-element.24.first_ref, f32[512,128]{1,0:T(8,128)S(1)} %get-tuple-element.25.second_ref), custom_call_target="tpu_custom_call" | custom-call | tf_op jit(solution)/shard_map/pallas_call | solution.py:342
  (18 shorter events, 0.1 us)
Async XLA Ops:
  1.6 24.4 %copy-start.3 = (bf16[2,128,128]{2,1,0:T(8,128)(2,1)S(1)}, bf16[2,128,128]{2,1,0:T(8,128)(2,1)}, u32[]{:S(2)}) copy-start(bf16[2,128,128]{2,1,0:T(8,128)(2,1)} %constant.10.clone.table_ref.forward_ref) | copy-start | bytes 196612
  26.1 19.5 %copy-start.1 = (bf16[2,2,256,256]{3,2,1,0:T(8,128)(2,1)S(1)}, bf16[2,2,256,256]{3,2,1,0:T(8,128)(2,1)}, u32[]{:S(2)}) copy-start(bf16[2,2,256,256]{3,2,1,0:T(8,128)(2,1)} %constant.12.clone.y_ref) | copy-start | bytes 1572868
  27.2 18.4 %copy-start = (bf16[2,2,256,256]{3,2,1,0:T(8,128)(2,1)S(1)}, bf16[2,2,256,256]{3,2,1,0:T(8,128)(2,1)}, u32[]{:S(2)}) copy-start(bf16[2,2,256,256]{3,2,1,0:T(8,128)(2,1)} %constant.13.clone.z_ref) | copy-start | bytes 1572868
  27.2 18.4 %all-to-all-start.1 = ((f32[32,16,128]{2,1,0:T(8,128)}), f32[32,16,128]{2,1,0:T(8,128)S(1)}, u32[]{:S(2)}, u32[]{:S(2)}) async-start(f32[32,16,128]{2,1,0:T(8,128)} %bitcast.3), calls=%async_computation.1 | async-start | bytes 524288 | tf_op jit(solution)/shard_map/all_to_all | solution.py:350
  36.7 0.7 collective-permute-start
  47.8 24.4 %copy-start.4 = (bf16[2,128,128]{2,1,0:T(8,128)(2,1)S(1)}, bf16[2,128,128]{2,1,0:T(8,128)(2,1)}, u32[]{:S(2)}) copy-start(bf16[2,128,128]{2,1,0:T(8,128)(2,1)} %constant.11.clone.inverse_ref) | copy-start | bytes 196612
  47.8 24.4 %all-to-all-start.2 = ((f32[32,24,128]{2,1,0:T(8,128)}), f32[32,24,128]{2,1,0:T(8,128)S(1)}, u32[]{:S(2)}, u32[]{:S(2)}) async-start(f32[32,24,128]{2,1,0:T(8,128)} %shard_map.97), calls=%async_computation.2 | async-start | bytes 786432 | tf_op jit(solution)/shard_map/all_to_all | solution.py:350
  51.7 8.1 %collective-permute-start.7 = (f32[128,128]{1,0:T(8,128)S(1)}, f32[128,128]{1,0:T(8,128)S(1)}, u32[]{:S(2)}, u32[]{:S(2)}) collective-permute-start(f32[128,128]{1,0:T(8,128)S(1)} %get-tuple-element.16.refs_0_.mask_ref), channel_id=1, source_target_pairs={{0,224},{32,0},{64,32},{96,64},{128,96},{160,128},{192,160},{224,1... | collective-permute-start | bytes 196616 | tf_op jit(solution)/shard_map/ppermute | solution.py:355
  51.8 9.2 %collective-permute-start.6 = (f32[128,128]{1,0:T(8,128)S(1)}, f32[128,128]{1,0:T(8,128)S(1)}, u32[]{:S(2)}, u32[]{:S(2)}) collective-permute-start(f32[128,128]{1,0:T(8,128)S(1)} %get-tuple-element.16.refs_0_.mask_ref), channel_id=1, source_target_pairs={{0,192},{32,224},{64,0},{96,32},{128,64},{160,96},{192,128},{224,1... | collective-permute-start | bytes 196616 | tf_op jit(solution)/shard_map/ppermute | solution.py:355
  52.4 8.7 %collective-permute-start.5 = (f32[128,128]{1,0:T(8,128)S(1)}, f32[128,128]{1,0:T(8,128)S(1)}, u32[]{:S(2)}, u32[]{:S(2)}) collective-permute-start(f32[128,128]{1,0:T(8,128)S(1)} %get-tuple-element.16.refs_0_.mask_ref), channel_id=1, source_target_pairs={{0,160},{32,192},{64,224},{96,0},{128,32},{160,64},{192,96},{224,1... | collective-permute-start | bytes 196616 | tf_op jit(solution)/shard_map/ppermute | solution.py:355
  55.0 7.0 %collective-permute-start.4 = (f32[128,128]{1,0:T(8,128)S(1)}, f32[128,128]{1,0:T(8,128)S(1)}, u32[]{:S(2)}, u32[]{:S(2)}) collective-permute-start(f32[128,128]{1,0:T(8,128)S(1)} %get-tuple-element.16.refs_0_.mask_ref), channel_id=1, source_target_pairs={{0,128},{32,160},{64,192},{96,224},{128,0},{160,32},{192,64},{224,... | collective-permute-start | bytes 196616 | tf_op jit(solution)/shard_map/ppermute | solution.py:355
  57.5 12.1 %collective-permute-start.3 = (f32[128,128]{1,0:T(8,128)S(1)}, f32[128,128]{1,0:T(8,128)S(1)}, u32[]{:S(2)}, u32[]{:S(2)}) collective-permute-start(f32[128,128]{1,0:T(8,128)S(1)} %get-tuple-element.16.refs_0_.mask_ref), channel_id=1, source_target_pairs={{0,96},{32,128},{64,160},{96,192},{128,224},{160,0},{192,32},{224,... | collective-permute-start | bytes 196616 | tf_op jit(solution)/shard_map/ppermute | solution.py:355
  59.8 9.7 %collective-permute-start.2 = (f32[128,128]{1,0:T(8,128)S(1)}, f32[128,128]{1,0:T(8,128)S(1)}, u32[]{:S(2)}, u32[]{:S(2)}) collective-permute-start(f32[128,128]{1,0:T(8,128)S(1)} %get-tuple-element.16.refs_0_.mask_ref), channel_id=1, source_target_pairs={{0,64},{32,96},{64,128},{96,160},{128,192},{160,224},{192,0},{224,... | collective-permute-start | bytes 196616 | tf_op jit(solution)/shard_map/ppermute | solution.py:355
  61.0 11.2 %collective-permute-start.1 = (f32[128,128]{1,0:T(8,128)S(1)}, f32[128,128]{1,0:T(8,128)S(1)}, u32[]{:S(2)}, u32[]{:S(2)}) collective-permute-start(f32[128,128]{1,0:T(8,128)S(1)} %get-tuple-element.16.refs_0_.mask_ref), channel_id=1, source_target_pairs={{0,32},{32,64},{64,96},{96,128},{128,160},{160,192},{192,224},{224... | collective-permute-start | bytes 196616 | tf_op jit(solution)/shard_map/ppermute | solution.py:355
  117.5 27.4 %copy-start.2 = (f32[8,16,4,128]{3,2,1,0:T(4,128)S(1)}, f32[8,16,4,128]{3,2,1,0:T(4,128)}, u32[]{:S(2)}) copy-start(f32[8,16,4,128]{3,2,1,0:T(4,128)} %param.8) | copy-start | bytes 786436

commit v6 on v5

--- a/solution.py
+++ b/solution.py
@@ -18,7 +18,7 @@
 DEPTH = GRID // SLABS
 ROWS = DEPTH * LINES
 BLOCK = PENCILS * 4 * LINES
-TARGETS = 4
+TARGETS = 2
 WIDTH = 8.0
 TILE = 8
 SMALLEST = 4e-7
@@ -82,11 +82,6 @@
     return dot(left[0], right[0]) + (dot(left[0], right[1]) + dot(left[1], right[0]))
 
 
-def full_product(left, right, dims):
-    dot = functools.partial(lax.dot_general, dimension_numbers=dims, preferred_element_type=F32)
-    return product(left, right, dims) + dot(left[1], right[1])
-
-
 def pair(ref, *index):
     return ref[(*index, 0)], ref[(*index, 1)]
 
@@ -241,7 +236,11 @@
     )
     start = 0
     for left, right in pairs:
-        sums = full_product(left, right, NT)
+        sums = product(left, right, NT)
+        rest = left[1].astype(F32)
+        rest = jnp.sum(rest * rest, axis=1, keepdims=True)
+        row, lane = [lax.broadcasted_iota(jnp.int32, sums.shape, axis) for axis in range(2)]
+        sums = sums + jnp.where(row == lane, rest, 0.0)
         out_ref[:, start : start + sums.shape[1]] = sums
         start += sums.shape[1]
 

time: 171 us -> 170 us (level)
  no operation moved by 1% of the time
where the time goes in v6:
time: 170 us
  blocking collectives  114 us (67%)
  starting transfers between devices  23.4 us (14%)
  waiting for transfers between devices  19.3 us (11%)
  Pallas kernels  12.7 us (7%)
    all_to_all x7, blocking collectives, exchange(): return lax.all_to_all(parts, axis, 0, 0, tiled=True)  114 us
    all_to_all x2, starting transfers between devices, exchange(): return lax.all_to_all(parts, axis, 0, 0, tiled=True)  13.4 us
    pallas_call x9, Pallas kernels, placed(): run(*[pltpu.with_memory_space_constraint(value, inputs) for value in valu...  12.7 us
    ppermute x7, waiting for transfers between devices, shifted(): return lax.ppermute(values, 'slab', ring)  11.2 us
    ppermute x7, starting transfers between devices, shifted(): return lax.ppermute(values, 'slab', ring)  9.29 us
    all_to_all x2, waiting for transfers between devices, exchange(): return lax.all_to_all(parts, axis, 0, 0, tiled=True)  8.18 us
  transfers between devices with their start and end apart: 10, of which 4 were waited for; matrix products, arithmetic and copies ran while one was open for 0% of the time, Pallas kernels for 0%

profile of v6, /device:TPU:1, one launch (start us, length us, event | category | flops | bytes accessed | tf_op | source)
XLA Modules:
  0.0 169.9 jit_solution(13427611788293137260)
XLA Ops:
  0.6 1.0 shard_map.95
  1.6 0.0 copy-start.3
  1.7 24.4 %all_to_all.45.staged_ref.last_ref = f32[8,120,128]{2,1,0:T(8,128)S(1)} all-to-all(f32[8,120,128]{2,1,0:T(8,128)S(1)} %get-tuple-element.15), channel_id=1, replica_groups=mesh['slab'=8,'pencil'=32] {'slab'}, dimensions={0} | all-to-all | bytes 983040 | tf_op jit(solution)/shard_map/all_to_all | solution.py:349
  26.1 1.1 shard_map.96
  27.2 9.5 %all-to-all-start.1 = ((f32[32,16,128]{2,1,0:T(8,128)}), f32[32,16,128]{2,1,0:T(8,128)S(1)}, u32[]{:S(2)}, u32[]{:S(2)}) async-start(f32[32,16,128]{2,1,0:T(8,128)} %bitcast.3), calls=%async_computation.1 | async-start | bytes 524288 | tf_op jit(solution)/shard_map/all_to_all | solution.py:349
  36.7 0.7 collective-permute-start
  37.3 0.0 collective-permute-done.edge_ref
  37.4 8.2 %all-to-all-done.1.in_ref = f32[32,16,128]{2,1,0:T(8,128)S(1)} async-done(((f32[32,16,128]{2,1,0:T(8,128)}), f32[32,16,128]{2,1,0:T(8,128)S(1)}, u32[]{:S(2)}, u32[]{:S(2)}) %all-to-all-start.1) | async-done | bytes 262176 | tf_op jit(solution)/shard_map/all_to_all | solution.py:349
  45.5 2.3 %shard_map.97 = f32[32,24,128]{2,1,0:T(8,128)} custom-call(f32[32,16,128]{2,1,0:T(8,128)S(1)} %all-to-all-done.1.in_ref, f32[8,120,128]{2,1,0:T(8,128)S(1)} %all_to_all.45.staged_ref.last_ref, f32[128,128]{1,0:T(8,128)S(1)} %collective-permute-done.edge_ref, bf16[2,2,256,256]{3,2,1,0:T(8,128)(2,1)S(1)} %copy-done.1, bf16[2,2,256,256]{3,2,1,0:T(8,128)(2,1)S(1)} %copy-done), custom_call_target="tpu_custom_call" | custom-call | tf_op jit(solution)/shard_map/pallas_call | solution.py:341
  47.8 3.9 %all-to-all-start.2 = ((f32[32,24,128]{2,1,0:T(8,128)}), f32[32,24,128]{2,1,0:T(8,128)S(1)}, u32[]{:S(2)}, u32[]{:S(2)}) async-start(f32[32,24,128]{2,1,0:T(8,128)} %shard_map.97), calls=%async_computation.2 | async-start | bytes 786432 | tf_op jit(solution)/shard_map/all_to_all | solution.py:349
  51.7 0.1 collective-permute-start.7
  51.8 0.6 collective-permute-start.6
  52.4 2.6 %collective-permute-start.5 = (f32[128,128]{1,0:T(8,128)S(1)}, f32[128,128]{1,0:T(8,128)S(1)}, u32[]{:S(2)}, u32[]{:S(2)}) collective-permute-start(f32[128,128]{1,0:T(8,128)S(1)} %get-tuple-element.16.refs_0_.mask_ref), channel_id=1, source_target_pairs={{0,160},{32,192},{64,224},{96,0},{128,32},{160,64},{192,96},{224,1... | collective-permute-start | bytes 196616 | tf_op jit(solution)/shard_map/ppermute | solution.py:354
  55.0 2.5 %collective-permute-start.4 = (f32[128,128]{1,0:T(8,128)S(1)}, f32[128,128]{1,0:T(8,128)S(1)}, u32[]{:S(2)}, u32[]{:S(2)}) collective-permute-start(f32[128,128]{1,0:T(8,128)S(1)} %get-tuple-element.16.refs_0_.mask_ref), channel_id=1, source_target_pairs={{0,128},{32,160},{64,192},{96,224},{128,0},{160,32},{192,64},{224,... | collective-permute-start | bytes 196616 | tf_op jit(solution)/shard_map/ppermute | solution.py:354
  57.5 2.4 %collective-permute-start.3 = (f32[128,128]{1,0:T(8,128)S(1)}, f32[128,128]{1,0:T(8,128)S(1)}, u32[]{:S(2)}, u32[]{:S(2)}) collective-permute-start(f32[128,128]{1,0:T(8,128)S(1)} %get-tuple-element.16.refs_0_.mask_ref), channel_id=1, source_target_pairs={{0,96},{32,128},{64,160},{96,192},{128,224},{160,0},{192,32},{224,... | collective-permute-start | bytes 196616 | tf_op jit(solution)/shard_map/ppermute | solution.py:354
  59.8 1.2 collective-permute-start.2
  61.1 1.0 collective-permute-done.4.refs_4_
  62.0 7.5 %collective-permute-done.3.refs_3_ = f32[128,128]{1,0:T(8,128)S(1)} collective-permute-done((f32[128,128]{1,0:T(8,128)S(1)}, f32[128,128]{1,0:T(8,128)S(1)}, u32[]{:S(2)}, u32[]{:S(2)}) %collective-permute-start.3) | collective-permute-done | bytes 65568 | tf_op jit(solution)/shard_map/ppermute | solution.py:354
  69.5 2.7 %collective-permute-done.1.refs_1_ = f32[128,128]{1,0:T(8,128)S(1)} collective-permute-done((f32[128,128]{1,0:T(8,128)S(1)}, f32[128,128]{1,0:T(8,128)S(1)}, u32[]{:S(2)}, u32[]{:S(2)}) %collective-permute-start.1) | collective-permute-done | bytes 65568 | tf_op jit(solution)/shard_map/ppermute | solution.py:354
  72.2 0.8 shard_map.98
  73.0 16.3 %all_to_all.46.in_ref = f32[32,16,128]{2,1,0:T(8,128)S(1)} all-to-all(f32[32,16,128]{2,1,0:T(8,128)S(1)} %bitcast.17), channel_id=1, replica_groups=mesh['slab'=8,'pencil'=32] {'pencil'}, dimensions={0} | all-to-all | bytes 524288 | tf_op jit(solution)/shard_map/all_to_all | solution.py:349
  89.3 1.5 shard_map.99
  90.8 12.4 %all_to_all.47 = f32[32,16,128]{2,1,0:T(8,128)S(1)} all-to-all(f32[32,16,128]{2,1,0:T(8,128)S(1)} %shard_map.99), channel_id=1, replica_groups=mesh['slab'=8,'pencil'=32] {'pencil'}, dimensions={0} | all-to-all | bytes 524288 | tf_op jit(solution)/shard_map/all_to_all | solution.py:349
  103.3 0.7 shard_map.100
  104.0 12.4 %all_to_all.48.in_ref = f32[32,16,128]{2,1,0:T(8,128)S(1)} all-to-all(f32[32,16,128]{2,1,0:T(8,128)S(1)} %bitcast.18), channel_id=1, replica_groups=mesh['slab'=8,'pencil'=32] {'pencil'}, dimensions={0} | all-to-all | bytes 524288 | tf_op jit(solution)/shard_map/all_to_all | solution.py:349
  116.4 1.0 shard_map.101
  117.5 0.0 copy-start.2
  117.5 27.4 %all_to_all.49 = f32[8,192,128]{2,1,0:T(8,128)S(1)} all-to-all(f32[8,192,128]{2,1,0:T(8,128)S(1)} %shard_map.101), channel_id=1, replica_groups=mesh['slab'=8,'pencil'=32] {'slab'}, dimensions={0} | all-to-all | bytes 1572864 | tf_op jit(solution)/shard_map/all_to_all | solution.py:349
  144.8 1.6 shard_map.102
  146.5 11.4 %all_to_all.50 = f32[32,8,128]{2,1,0:T(8,128)S(1)} all-to-all(f32[32,8,128]{2,1,0:T(8,128)S(1)} %broadcast_in_dim.4), channel_id=1, replica_groups=mesh['slab'=8,'pencil'=32] {'pencil'}, dimensions={0} | all-to-all | bytes 262144 | tf_op jit(solution)/shard_map/all_to_all | solution.py:349
  158.0 9.2 %all_to_all.51.sums_ref = f32[8,8,128]{2,1,0:T(8,128)S(1)} all-to-all(f32[8,8,128]{2,1,0:T(8,128)S(1)} %broadcast_in_dim.5), channel_id=1, replica_groups=mesh['slab'=8,'pencil'=32] {'slab'}, dimensions={0} | all-to-all | bytes 65536 | tf_op jit(solution)/shard_map/all_to_all | solution.py:349
  167.2 2.6 %shard_map.103 = (f32[512,128]{1,0:T(8,128)}, f32[64,128]{1,0:T(8,128)}) custom-call(f32[8,8,128]{2,1,0:T(8,128)S(1)} %all_to_all.51.sums_ref, f32[8,128]{1,0:T(8,128)S(1)} %get-tuple-element.19.shift_ref, f32[512,128]{1,0:T(8,128)S(1)} %bitcast.15, f32[512,128]{1,0:T(8,128)S(1)} %get-tuple-element.24.first_ref, f32[512,128]{1,0:T(8,128)S(1)} %get-tuple-element.25.second_ref), custom_call_target="tpu_custom_call" | custom-call | tf_op jit(solution)/shard_map/pallas_call | solution.py:341
  (18 shorter events, 0.1 us)
Async XLA Ops:
  1.6 24.4 %copy-start.3 = (bf16[2,128,128]{2,1,0:T(8,128)(2,1)S(1)}, bf16[2,128,128]{2,1,0:T(8,128)(2,1)}, u32[]{:S(2)}) copy-start(bf16[2,128,128]{2,1,0:T(8,128)(2,1)} %constant.10.clone.table_ref.forward_ref) | copy-start | bytes 196612
  26.1 19.5 %copy-start.1 = (bf16[2,2,256,256]{3,2,1,0:T(8,128)(2,1)S(1)}, bf16[2,2,256,256]{3,2,1,0:T(8,128)(2,1)}, u32[]{:S(2)}) copy-start(bf16[2,2,256,256]{3,2,1,0:T(8,128)(2,1)} %constant.12.clone.y_ref) | copy-start | bytes 1572868
  27.2 18.4 %copy-start = (bf16[2,2,256,256]{3,2,1,0:T(8,128)(2,1)S(1)}, bf16[2,2,256,256]{3,2,1,0:T(8,128)(2,1)}, u32[]{:S(2)}) copy-start(bf16[2,2,256,256]{3,2,1,0:T(8,128)(2,1)} %constant.13.clone.z_ref) | copy-start | bytes 1572868
  27.2 18.4 %all-to-all-start.1 = ((f32[32,16,128]{2,1,0:T(8,128)}), f32[32,16,128]{2,1,0:T(8,128)S(1)}, u32[]{:S(2)}, u32[]{:S(2)}) async-start(f32[32,16,128]{2,1,0:T(8,128)} %bitcast.3), calls=%async_computation.1 | async-start | bytes 524288 | tf_op jit(solution)/shard_map/all_to_all | solution.py:349
  36.7 0.7 collective-permute-start
  47.8 24.4 %copy-start.4 = (bf16[2,128,128]{2,1,0:T(8,128)(2,1)S(1)}, bf16[2,128,128]{2,1,0:T(8,128)(2,1)}, u32[]{:S(2)}) copy-start(bf16[2,128,128]{2,1,0:T(8,128)(2,1)} %constant.11.clone.inverse_ref) | copy-start | bytes 196612
  47.8 24.4 %all-to-all-start.2 = ((f32[32,24,128]{2,1,0:T(8,128)}), f32[32,24,128]{2,1,0:T(8,128)S(1)}, u32[]{:S(2)}, u32[]{:S(2)}) async-start(f32[32,24,128]{2,1,0:T(8,128)} %shard_map.97), calls=%async_computation.2 | async-start | bytes 786432 | tf_op jit(solution)/shard_map/all_to_all | solution.py:349
  51.7 8.1 %collective-permute-start.7 = (f32[128,128]{1,0:T(8,128)S(1)}, f32[128,128]{1,0:T(8,128)S(1)}, u32[]{:S(2)}, u32[]{:S(2)}) collective-permute-start(f32[128,128]{1,0:T(8,128)S(1)} %get-tuple-element.16.refs_0_.mask_ref), channel_id=1, source_target_pairs={{0,224},{32,0},{64,32},{96,64},{128,96},{160,128},{192,160},{224,1... | collective-permute-start | bytes 196616 | tf_op jit(solution)/shard_map/ppermute | solution.py:354
  51.8 9.2 %collective-permute-start.6 = (f32[128,128]{1,0:T(8,128)S(1)}, f32[128,128]{1,0:T(8,128)S(1)}, u32[]{:S(2)}, u32[]{:S(2)}) collective-permute-start(f32[128,128]{1,0:T(8,128)S(1)} %get-tuple-element.16.refs_0_.mask_ref), channel_id=1, source_target_pairs={{0,192},{32,224},{64,0},{96,32},{128,64},{160,96},{192,128},{224,1... | collective-permute-start | bytes 196616 | tf_op jit(solution)/shard_map/ppermute | solution.py:354
  52.4 8.7 %collective-permute-start.5 = (f32[128,128]{1,0:T(8,128)S(1)}, f32[128,128]{1,0:T(8,128)S(1)}, u32[]{:S(2)}, u32[]{:S(2)}) collective-permute-start(f32[128,128]{1,0:T(8,128)S(1)} %get-tuple-element.16.refs_0_.mask_ref), channel_id=1, source_target_pairs={{0,160},{32,192},{64,224},{96,0},{128,32},{160,64},{192,96},{224,1... | collective-permute-start | bytes 196616 | tf_op jit(solution)/shard_map/ppermute | solution.py:354
  55.0 7.0 %collective-permute-start.4 = (f32[128,128]{1,0:T(8,128)S(1)}, f32[128,128]{1,0:T(8,128)S(1)}, u32[]{:S(2)}, u32[]{:S(2)}) collective-permute-start(f32[128,128]{1,0:T(8,128)S(1)} %get-tuple-element.16.refs_0_.mask_ref), channel_id=1, source_target_pairs={{0,128},{32,160},{64,192},{96,224},{128,0},{160,32},{192,64},{224,... | collective-permute-start | bytes 196616 | tf_op jit(solution)/shard_map/ppermute | solution.py:354
  57.5 12.1 %collective-permute-start.3 = (f32[128,128]{1,0:T(8,128)S(1)}, f32[128,128]{1,0:T(8,128)S(1)}, u32[]{:S(2)}, u32[]{:S(2)}) collective-permute-start(f32[128,128]{1,0:T(8,128)S(1)} %get-tuple-element.16.refs_0_.mask_ref), channel_id=1, source_target_pairs={{0,96},{32,128},{64,160},{96,192},{128,224},{160,0},{192,32},{224,... | collective-permute-start | bytes 196616 | tf_op jit(solution)/shard_map/ppermute | solution.py:354
  59.8 9.7 %collective-permute-start.2 = (f32[128,128]{1,0:T(8,128)S(1)}, f32[128,128]{1,0:T(8,128)S(1)}, u32[]{:S(2)}, u32[]{:S(2)}) collective-permute-start(f32[128,128]{1,0:T(8,128)S(1)} %get-tuple-element.16.refs_0_.mask_ref), channel_id=1, source_target_pairs={{0,64},{32,96},{64,128},{96,160},{128,192},{160,224},{192,0},{224,... | collective-permute-start | bytes 196616 | tf_op jit(solution)/shard_map/ppermute | solution.py:354
  61.0 11.2 %collective-permute-start.1 = (f32[128,128]{1,0:T(8,128)S(1)}, f32[128,128]{1,0:T(8,128)S(1)}, u32[]{:S(2)}, u32[]{:S(2)}) collective-permute-start(f32[128,128]{1,0:T(8,128)S(1)} %get-tuple-element.16.refs_0_.mask_ref), channel_id=1, source_target_pairs={{0,32},{32,64},{64,96},{96,128},{128,160},{160,192},{192,224},{224... | collective-permute-start | bytes 196616 | tf_op jit(solution)/shard_map/ppermute | solution.py:354
  117.5 27.4 %copy-start.2 = (f32[8,16,4,128]{3,2,1,0:T(4,128)S(1)}, f32[8,16,4,128]{3,2,1,0:T(4,128)}, u32[]{:S(2)}) copy-start(f32[8,16,4,128]{3,2,1,0:T(4,128)} %param.8) | copy-start | bytes 786436
